TPU v7x, 32 devices: a 4x4x1 block of a 4x4x8 slice. The times are simulated.
32 devices in a mesh: dp: 1 (over z), tp: 4 (over y), cp: 8 (over x, core).
Axes of the slice: x: 4, y: 4, z: 1, core: 2. Of those that a mesh axis runs over, the one named last changes fastest.
The devices are a block of a 4x4x8 slice.
Arguments:
- x_in: bfloat16 [2, 4096, 3072], P('dp', 'cp')
- w_q: bfloat16 [3072, 24, 128], P(None, 'tp')
- w_k: bfloat16 [3072, 8, 128], P(None, 'tp')
- w_v: bfloat16 [3072, 8, 128], P(None, 'tp')
- w_o: bfloat16 [24, 128, 3072], P('tp')
- q_norm_w: float32 [24, 128], P('tp')
- k_norm_w: float32 [8, 128], P('tp')
- post_norm_w: float32 [3072], replicated
- grad_y: bfloat16 [2, 4096, 3072], P('dp', 'cp')
Outputs:
- output 1: bfloat16 [2, 4096, 3072], P('dp', 'cp')
- output 2: bfloat16 [2, 4096, 3072], P('dp', 'cp')
- output 3: float32 [3072, 24, 128], P('dp', 'tp')
- output 4: float32 [3072, 8, 128], P('dp', 'tp')
- output 5: float32 [3072, 8, 128], P('dp', 'tp')
- output 6: float32 [24, 128, 3072], P(('dp', 'tp'))
- output 7: float32 [24, 128], P(('dp', 'tp'))
- output 8: float32 [8, 128], P(('dp', 'tp'))
- output 9: float32 [3072], P('dp')
All inputs are finite; a program needn't handle non-finite values.
Results may differ from a plain program's by a relative error of at most 0.016555.
Values are sent between devices in bfloat16 or wider.
A program may use at most 768 MiB of HBM per device.

v0:
```python
import jax
import jax.numpy as jnp
from jax import lax
from jax.sharding import PartitionSpec as P

ROPE_THETA = 500000.0
NORM_EPS = 1e-6
MASK_VALUE = -1e30


def rope_tables(start_pos, seq_rows, head_dim):
    half_dim = head_dim // 2
    inv_freq = ROPE_THETA ** (-2.0 * jnp.arange(half_dim, dtype=jnp.float32) / head_dim)
    positions = (start_pos + jnp.arange(seq_rows)).astype(jnp.float32)
    angles = positions[:, None] * inv_freq[None, :]
    return jnp.cos(angles), jnp.sin(angles)


def apply_rope(values, cos_tab, sin_tab):
    half_dim = values.shape[-1] // 2
    low_half = values[..., :half_dim]
    high_half = values[..., half_dim:]
    cos_rows = cos_tab[:, None, :]
    sin_rows = sin_tab[:, None, :]
    return jnp.concatenate([low_half * cos_rows - high_half * sin_rows, high_half * cos_rows + low_half * sin_rows], axis=-1)


def rope_back(grad_in, cos_tab, sin_tab):
    half_dim = grad_in.shape[-1] // 2
    low_half = grad_in[..., :half_dim]
    high_half = grad_in[..., half_dim:]
    cos_rows = cos_tab[:, None, :]
    sin_rows = sin_tab[:, None, :]
    return jnp.concatenate([low_half * cos_rows + high_half * sin_rows, high_half * cos_rows - low_half * sin_rows], axis=-1)


def whole_norm(lin_out, weight, width):
    sq_sum = lax.psum(jnp.sum(lin_out * lin_out, axis=(2, 3)), "tp")
    inv_rms = lax.rsqrt(sq_sum / width + NORM_EPS)[:, :, None, None]
    normed = lin_out * inv_rms
    return normed * weight, normed, inv_rms


def whole_norm_back(grad_out, normed, inv_rms, weight, width):
    grad_weight = jnp.sum(grad_out * normed, axis=(0, 1))
    grad_normed = grad_out * weight
    dot_sum = lax.psum(jnp.sum(grad_normed * normed, axis=(2, 3)), "tp")
    grad_lin = inv_rms * (grad_normed - normed * (dot_sum / width)[:, :, None, None])
    return grad_lin, grad_weight


def attend_block(q_rot, k_blk, v_blk, stats_in, score_scale, causal):
    row_max, row_sum, out_acc = stats_in
    scores = jnp.einsum("blkgd,bmkd->bklgm", q_rot, k_blk, preferred_element_type=jnp.float32) * score_scale
    if causal:
        block_len = q_rot.shape[1]
        lower_tri = jnp.arange(block_len)[:, None] >= jnp.arange(block_len)[None, :]
        scores = jnp.where(lower_tri[:, None, :], scores, MASK_VALUE)
    new_max = jnp.maximum(row_max, jnp.max(scores, axis=-1))
    prob_blk = jnp.exp(scores - new_max[..., None])
    rescale = jnp.exp(row_max - new_max)
    new_sum = row_sum * rescale + jnp.sum(prob_blk, axis=-1)
    new_acc = out_acc * rescale[..., None] + jnp.einsum("bklgm,bmkd->bklgd", prob_blk.astype(jnp.bfloat16), v_blk, preferred_element_type=jnp.float32)
    return new_max, new_sum, new_acc


def attend_block_back(q_rot, k_blk, v_blk, grad_o, log_sum, row_delta, score_scale, causal):
    scores = jnp.einsum("blkgd,bmkd->bklgm", q_rot, k_blk, preferred_element_type=jnp.float32) * score_scale
    if causal:
        block_len = q_rot.shape[1]
        lower_tri = jnp.arange(block_len)[:, None] >= jnp.arange(block_len)[None, :]
        scores = jnp.where(lower_tri[:, None, :], scores, MASK_VALUE)
    prob_blk = jnp.exp(scores - log_sum[..., None])
    grad_v = jnp.einsum("bklgm,blkgd->bkmd", prob_blk.astype(jnp.bfloat16), grad_o, preferred_element_type=jnp.float32)
    grad_p = jnp.einsum("blkgd,bmkd->bklgm", grad_o, v_blk, preferred_element_type=jnp.float32)
    grad_s = (prob_blk * (grad_p - row_delta[..., None]) * score_scale).astype(jnp.bfloat16)
    grad_q = jnp.einsum("bklgm,bmkd->bklgd", grad_s, k_blk, preferred_element_type=jnp.float32)
    grad_k = jnp.einsum("bklgm,blkgd->bkmd", grad_s, q_rot, preferred_element_type=jnp.float32)
    return grad_q, grad_k, grad_v


def solution(mesh):
    tp_size = mesh.shape["tp"]
    cp_size = mesh.shape["cp"]
    perm_next = [(src_dev, (src_dev + 1) % cp_size) for src_dev in range(cp_size)]
    act_spec = P("dp", "cp", None)
    col_spec = P(None, "tp", None)
    part_col = P("dp", "tp", None)
    in_specs = (act_spec, col_spec, col_spec, col_spec, P("tp", None, None), P("tp", None), P("tp", None), P(None), act_spec)
    out_specs = (act_spec, act_spec, part_col, part_col, part_col, P(("dp", "tp"), None, None), P(("dp", "tp"), None), P(("dp", "tp"), None), P("dp"))

    def local_run(x_in, w_q, w_k, w_v, w_o, q_norm_w, k_norm_w, post_norm_w, grad_y):
        n_batch = x_in.shape[0]
        block_len = x_in.shape[1]
        heads_loc = w_q.shape[1]
        kv_loc = w_k.shape[1]
        head_dim = w_q.shape[2]
        group_size = heads_loc // kv_loc
        q_width = heads_loc * head_dim * tp_size
        k_width = kv_loc * head_dim * tp_size
        score_scale = head_dim ** -0.5
        cp_index = lax.axis_index("cp")
        cos_tab, sin_tab = rope_tables(cp_index * block_len, block_len, head_dim)

        q_lin = jnp.einsum("bld,dhe->blhe", x_in, w_q, preferred_element_type=jnp.float32)
        k_lin = jnp.einsum("bld,dhe->blhe", x_in, w_k, preferred_element_type=jnp.float32)
        v_lin = jnp.einsum("bld,dhe->blhe", x_in, w_v, preferred_element_type=jnp.float32)
        q_scaled, q_hat, q_inv = whole_norm(q_lin, q_norm_w, q_width)
        k_scaled, k_hat, k_inv = whole_norm(k_lin, k_norm_w, k_width)
        q_rot = apply_rope(q_scaled, cos_tab, sin_tab).astype(jnp.bfloat16).reshape(n_batch, block_len, kv_loc, group_size, head_dim)
        k_rot = apply_rope(k_scaled, cos_tab, sin_tab).astype(jnp.bfloat16)
        v_val = v_lin.astype(jnp.bfloat16)

        stat_shape = (n_batch, kv_loc, block_len, group_size)
        first_state = (jnp.full(stat_shape, MASK_VALUE, jnp.float32), jnp.zeros(stat_shape, jnp.float32), jnp.zeros(stat_shape + (head_dim,), jnp.float32))
        soft_state = attend_block(q_rot, k_rot, v_val, first_state, score_scale, True)

        def fwd_step(step_idx, loop_state):
            k_cur, v_cur, stats_in = loop_state
            k_cur, v_cur = lax.ppermute((k_cur, v_cur), "cp", perm_next)

            def use_block(stats_now):
                return attend_block(q_rot, k_cur, v_cur, stats_now, score_scale, False)

            def keep_block(stats_now):
                return stats_now

            stats_out = lax.cond(step_idx <= cp_index, use_block, keep_block, stats_in)
            return k_cur, v_cur, stats_out

        row_max, row_sum, out_acc = lax.fori_loop(1, cp_size, fwd_step, (k_rot, v_val, soft_state))[2]
        attn_out = (out_acc / row_sum[..., None]).astype(jnp.bfloat16).transpose(0, 2, 1, 3, 4).reshape(n_batch, block_len, heads_loc, head_dim)
        log_sum = row_max + jnp.log(row_sum)

        proj = lax.psum(jnp.einsum("blhe,hed->bld", attn_out, w_o, preferred_element_type=jnp.float32), "tp")
        post_inv = lax.rsqrt(jnp.mean(proj * proj, axis=-1, keepdims=True) + NORM_EPS)
        post_hat = proj * post_inv
        y_out = (x_in + post_hat * post_norm_w).astype(jnp.bfloat16)

        grad_f = grad_y.astype(jnp.float32)
        grad_post = jnp.sum(grad_f * post_hat, axis=(0, 1))
        grad_hat = grad_f * post_norm_w
        grad_proj = (post_inv * (grad_hat - post_hat * jnp.mean(grad_hat * post_hat, axis=-1, keepdims=True))).astype(jnp.bfloat16)
        grad_w_o = jnp.einsum("blhe,bld->hed", attn_out, grad_proj, preferred_element_type=jnp.float32)
        grad_attn = jnp.einsum("bld,hed->blhe", grad_proj, w_o, preferred_element_type=jnp.float32)
        row_delta = jnp.sum(grad_attn * attn_out, axis=-1).reshape(n_batch, block_len, kv_loc, group_size).transpose(0, 2, 1, 3)
        grad_o = grad_attn.astype(jnp.bfloat16).reshape(n_batch, block_len, kv_loc, group_size, head_dim)

        diag_q, diag_k, diag_v = attend_block_back(q_rot, k_rot, v_val, grad_o, log_sum, row_delta, score_scale, True)

        def bwd_step(step_idx, loop_state):
            k_cur, v_cur, dk_cur, dv_cur, dq_cur = loop_state
            k_cur, v_cur, dk_cur, dv_cur = lax.ppermute((k_cur, v_cur, dk_cur, dv_cur), "cp", perm_next)

            def use_block(acc_in):
                part_q, part_k, part_v = attend_block_back(q_rot, k_cur, v_cur, grad_o, log_sum, row_delta, score_scale, False)
                return acc_in[0] + part_q, acc_in[1] + part_k, acc_in[2] + part_v

            def keep_block(acc_in):
                return acc_in

            dq_cur, dk_cur, dv_cur = lax.cond(step_idx <= cp_index, use_block, keep_block, (dq_cur, dk_cur, dv_cur))
            return k_cur, v_cur, dk_cur, dv_cur, dq_cur

        back_state = lax.fori_loop(1, cp_size, bwd_step, (k_rot, v_val, diag_k, diag_v, diag_q))
        dk_home, dv_home = lax.ppermute((back_state[2], back_state[3]), "cp", perm_next)
        grad_q_rot = back_state[4].transpose(0, 2, 1, 3, 4).reshape(n_batch, block_len, heads_loc, head_dim)
        grad_k_rot = dk_home.transpose(0, 2, 1, 3)
        grad_v16 = dv_home.transpose(0, 2, 1, 3).astype(jnp.bfloat16)

        grad_q_lin, grad_q_norm = whole_norm_back(rope_back(grad_q_rot, cos_tab, sin_tab), q_hat, q_inv, q_norm_w, q_width)
        grad_k_lin, grad_k_norm = whole_norm_back(rope_back(grad_k_rot, cos_tab, sin_tab), k_hat, k_inv, k_norm_w, k_width)
        grad_q16 = grad_q_lin.astype(jnp.bfloat16)
        grad_k16 = grad_k_lin.astype(jnp.bfloat16)
        grad_w_q = jnp.einsum("bld,blhe->dhe", x_in, grad_q16, preferred_element_type=jnp.float32)
        grad_w_k = jnp.einsum("bld,blhe->dhe", x_in, grad_k16, preferred_element_type=jnp.float32)
        grad_w_v = jnp.einsum("bld,blhe->dhe", x_in, grad_v16, preferred_element_type=jnp.float32)
        grad_x_part = (jnp.einsum("blhe,dhe->bld", grad_q16, w_q, preferred_element_type=jnp.float32)
                       + jnp.einsum("blhe,dhe->bld", grad_k16, w_k, preferred_element_type=jnp.float32)
                       + jnp.einsum("blhe,dhe->bld", grad_v16, w_v, preferred_element_type=jnp.float32))
        grad_x = (grad_f + lax.psum(grad_x_part, "tp")).astype(jnp.bfloat16)
        weight_grads = lax.psum((grad_w_q, grad_w_k, grad_w_v, grad_w_o, grad_q_norm, grad_k_norm, grad_post), "cp")
        return (y_out, grad_x) + tuple(weight_grads)

    return jax.shard_map(local_run, mesh=mesh, in_specs=in_specs, out_specs=out_specs, check_vma=False)
```

profile of v0, /device:TPU:97, one launch (start us, length us, event | category | flops | bytes accessed | tf_op | source)
XLA Modules:
  0.0 1600.9 jit_solution(11627413543204524143)
XLA Ops:
  7.4 5.9 fusion.91
  21.0 10.1 multiply_reduce_fusion.5
  31.7 11.3 all-reduce.3
  62.8 6.4 fusion.77
  69.2 172.1 %while.42 = (s32[]{:T(128)}, bf16[2,512,2,128]{3,1,2,0:T(8,128)(2,1)S(1)}, bf16[2,512,2,128]{3,1,2,0:T(8,128)(2,1)S(1)}, f32[2,2,512,3]{2,3,1,0:T(4,128)S(1)}, f...) while((s32[]{:T(128)}, ...), condition=%wide.region_11.12_spmd, body=%wide.region_6.11_spmd.sunk | while | flops 1637363712 | bytes 78709136 | solution.py:131
  73.1 6.0 collective-permute-done.1
  79.1 5.6 collective-permute-done
  84.7 15.3 conditional.4
  103.7 6.1 collective-permute-done.1
  109.7 5.6 collective-permute-done
  116.4 17.8 %collective-permute-start.1 = (bf16[2,512,2,128]{3,1,2,0:T(8,128)(2,1)S(1)}, bf16[2,512,2,128]{3,1,2,0:T(8,128)(2,1)S(1)}, u32[]{:S(2)}, u32[]{:S(2)}) collective-permute-start(bf16[2,512,2,128]{3,1,2,0:T(8,128)(2,1)S(1)} %get-tuple-element.735), channel_id=1, source_target_pairs={{0,1},{1,2},{2,3},{3,4},{4,5},{5,6},{6,7},{7,0},{8,9},{9,10},{10,1... | collective-permute-start | bytes 1572872 | tf_op jit(solution)/shard_map/while/body/eval_jaxpr/ppermute | solution.py:120
  134.3 6.1 collective-permute-done.1
  140.4 5.6 collective-permute-done
  149.6 14.6 collective-permute-start
  164.2 6.1 collective-permute-done
  173.8 5.6 collective-permute-start
  180.0 5.6 collective-permute-done
  186.7 13.3 collective-permute-start.1
  199.9 10.2 collective-permute-start
  210.1 6.1 collective-permute-done
  219.8 14.3 collective-permute-start
  234.1 6.1 collective-permute-done
  245.0 9.6 convolution_bitcast_fusion.1
  259.5 249.4 %all-reduce.8.cloned.1.call-done = f32[2,512,3072]{2,1,0:T(8,128)} async-done(((f32[2,512,3072]{2,1,0:T(8,128)}), f32[2,512,3072]{2,1,0:T(8,128)}) %all-reduce.8.cloned.1.call-update) | async-done | bytes 12582928 | tf_op jit(solution)/shard_map/psum | solution.py:135
  508.9 5.6 multiply_reduce_fusion.1
  517.1 7.1 fusion.35
  524.3 10.7 fusion.42
  542.2 8.3 fusion.88
  550.4 7.3 multiply_convert_fusion.1
  564.5 7.6 convolution_bitcast_fusion.2
  572.1 402.8 %while.43 = (s32[]{:T(128)}, bf16[2,512,2,128]{3,1,2,0:T(8,128)(2,1)}, bf16[2,512,2,128]{3,1,2,0:T(8,128)(2,1)}, f32[2,2,512,128]{3,2,1,0:T(8,128)}, f32[2,2,512...) while((s32[]{:T(128)}, ...), condition=%wide.region_19.0_spmd, body=%wide.region_16.19_spmd.sunk | while | flops 4056154112 | bytes 125379064 | solution.py:165
  576.0 26.9 %collective-permute-done.3 = bf16[2,512,2,128]{3,1,2,0:T(8,128)(2,1)} collective-permute-done((bf16[2,512,2,128]{3,1,2,0:T(8,128)(2,1)}, bf16[2,512,2,128]{3,1,2,0:T(8,128)(2,1)}, u32[]{:S(2)}, u32[]{:S(2)}) %collective-permute-start.3) | collective-permute-done | bytes 524320 | tf_op jit(solution)/shard_map/while/body/eval_jaxpr/ppermute | solution.py:153
  609.3 28.4 %conditional.5 = ((f32[2,2,512,3,128]{4,2,3,1,0:T(8,128)}, f32[2,2,512,128]{3,2,1,0:T(8,128)}, f32[2,2,512,128]{3,2,1,0:T(8,128)S(1)})) conditional(s32[]{:T(128)} %convert_element_type.163, (f32[2,2,512,3,128]{4,2,3,1,0:T(8,128)}, f32[2,2,512,128]{3,2,1,0:T(8,128)}, f32[2,2,512,128]{3,2,1,0:T(8,128)S(1)}) %tuple.101, ...), branch_computations={%region_17.17_spmd, %region_18.18_spmd} | conditional | flops 4056154112 | bytes 106504312 | solution.py:162
  609.3 6.4 fusion.26
  615.7 7.0 fusion.20
  622.7 7.1 multiply_convert_fusion
  645.1 26.9 %collective-permute-done.3 = bf16[2,512,2,128]{3,1,2,0:T(8,128)(2,1)} collective-permute-done((bf16[2,512,2,128]{3,1,2,0:T(8,128)(2,1)}, bf16[2,512,2,128]{3,1,2,0:T(8,128)(2,1)}, u32[]{:S(2)}, u32[]{:S(2)}) %collective-permute-start.3) | collective-permute-done | bytes 524320 | tf_op jit(solution)/shard_map/while/body/eval_jaxpr/ppermute | solution.py:153
  681.8 30.9 %collective-permute-start.5 = (f32[2,2,512,128]{3,2,1,0:T(8,128)}, f32[2,2,512,128]{3,2,1,0:T(8,128)S(1)}, u32[]{:S(2)}, u32[]{:S(2)}) collective-permute-start(f32[2,2,512,128]{3,2,1,0:T(8,128)} %get-tuple-element.767), channel_id=1, source_target_pairs={{0,1},{1,2},{2,3},{3,4},{4,5},{5,6},{6,7},{7,0},{8,9},{9,10},{10,1... | collective-permute-start | bytes 3145736 | tf_op jit(solution)/shard_map/while/body/eval_jaxpr/ppermute | solution.py:153
  714.3 27.0 %collective-permute-done.3 = bf16[2,512,2,128]{3,1,2,0:T(8,128)(2,1)} collective-permute-done((bf16[2,512,2,128]{3,1,2,0:T(8,128)(2,1)}, bf16[2,512,2,128]{3,1,2,0:T(8,128)(2,1)}, u32[]{:S(2)}, u32[]{:S(2)}) %collective-permute-start.3) | collective-permute-done | bytes 524320 | tf_op jit(solution)/shard_map/while/body/eval_jaxpr/ppermute | solution.py:153
  753.5 27.5 %collective-permute-start.4 = (f32[2,2,512,128]{3,2,1,0:T(8,128)}, f32[2,2,512,128]{3,2,1,0:T(8,128)}, u32[]{:S(2)}, u32[]{:S(2)}) collective-permute-start(f32[2,2,512,128]{3,2,1,0:T(8,128)} %get-tuple-element.766), channel_id=1, source_target_pairs={{0,1},{1,2},{2,3},{3,4},{4,5},{5,6},{6,7},{7,0},{8,9},{9,10},{10,1... | collective-permute-start | bytes 3145736 | tf_op jit(solution)/shard_map/while/body/eval_jaxpr/ppermute | solution.py:153
  783.6 14.8 collective-permute-done.3
  810.6 11.2 collective-permute-start.4
  821.8 30.9 %collective-permute-start.3 = (bf16[2,512,2,128]{3,1,2,0:T(8,128)(2,1)}, bf16[2,512,2,128]{3,1,2,0:T(8,128)(2,1)}, u32[]{:S(2)}, u32[]{:S(2)}) collective-permute-start(bf16[2,512,2,128]{3,1,2,0:T(8,128)(2,1)} %get-tuple-element.765), channel_id=1, source_target_pairs={{0,1},{1,2},{2,3},{3,4},{4,5},{5,6},{6,7},{7,0},{8,9},{9,10},{10,1... | collective-permute-start | bytes 1572872 | tf_op jit(solution)/shard_map/while/body/eval_jaxpr/ppermute | solution.py:153
  852.8 6.1 collective-permute-done.3
  871.1 20.0 %collective-permute-start.4 = (f32[2,2,512,128]{3,2,1,0:T(8,128)}, f32[2,2,512,128]{3,2,1,0:T(8,128)}, u32[]{:S(2)}, u32[]{:S(2)}) collective-permute-start(f32[2,2,512,128]{3,2,1,0:T(8,128)} %get-tuple-element.766), channel_id=1, source_target_pairs={{0,1},{1,2},{2,3},{3,4},{4,5},{5,6},{6,7},{7,0},{8,9},{9,10},{10,1... | collective-permute-start | bytes 3145736 | tf_op jit(solution)/shard_map/while/body/eval_jaxpr/ppermute | solution.py:153
  893.6 27.2 %collective-permute-start.2 = (bf16[2,512,2,128]{3,1,2,0:T(8,128)(2,1)}, bf16[2,512,2,128]{3,1,2,0:T(8,128)(2,1)S(1)}, u32[]{:S(2)}, u32[]{:S(2)}) collective-permute-start(bf16[2,512,2,128]{3,1,2,0:T(8,128)(2,1)} %get-tuple-element.764), channel_id=1, source_target_pairs={{0,1},{1,2},{2,3},{3,4},{4,5},{5,6},{6,7},{7,0},{8,9},{9,10},{10,1... | collective-permute-start | bytes 1572872 | tf_op jit(solution)/shard_map/while/body/eval_jaxpr/ppermute | solution.py:153
  933.5 14.4 collective-permute-start.4
  950.3 11.2 collective-permute-start.2
  979.6 23.6 %collective-permute-start.7 = (bf16[2,2,512,128]{3,2,1,0:T(8,128)(2,1)}, bf16[2,2,512,128]{3,2,1,0:T(8,128)(2,1)}, u32[]{:S(2)}, u32[]{:S(2)}) collective-permute-start(bf16[2,2,512,128]{3,2,1,0:T(8,128)(2,1)} %convert.30), channel_id=1, source_target_pairs={{0,1},{1,2},{2,3},{3,4},{4,5},{5,6},{6,7},{7,0},{8,9},{9,10},{10,1... | collective-permute-start | bytes 1572872 | tf_op jit(solution)/shard_map/ppermute | solution.py:166
  1003.1 9.8 collective-permute-start.6
  1029.4 6.6 all-reduce.2
  1040.6 6.8 fusion.71
  1047.5 7.4 fusion.62
  1056.4 6.4 fusion.80
  1062.8 10.8 fusion.68
  1073.6 14.7 bitcast_add_fusion
  1089.0 61.8 %all-reduce = (f32[6,128]{1,0:T(8,128)}, f32[2,128]{1,0:T(2,128)}, f32[3072]{0:T(1024)}) all-reduce(f32[6,128]{1,0:T(8,128)S(1)} %get-tuple-element.503, f32[2,128]{1,0:T(2,128)S(1)} %get-tuple-element.505, f32[3072]{0:T(1024)S(1)} %copy-done.44), channel_id=1, replica_groups=mesh['dp'=1,'tp'=4,'cp'=8] {'cp'}, use_global_device_ids=true, to_apply=%region_30.31 | all-reduce | flops 4096 | bytes 32768 | tf_op jit(solution)/shard_map/psum | solution.py:182
  1150.8 198.1 %all-reduce.12.cloned.1.call-done = (f32[3072,6,128]{0,2,1:T(8,128)}, f32[3072,2,128]{0,2,1:T(8,128)}, f32[3072,2,128]{0,2,1:T(8,128)}, f32[6,128,3072]{2,1,0:T(8,128)}) async-done(((f32[3072,6,128]{0,2,1:T(8,128)}, f32[3072,2,128]{0,2,1:T(8,128)}, f32[3072,2,128]{0,2,1:T(8,128)}, f32[6,128,3072]{2,1,0:T(8,128)}), (f32[3072,6,128]{0,2,1:T(8,128)}, f32[3072,2,128]{0,2,1:T(8,128)}, f32[3072,2,128]{0,2,1:T(8,128)}, ...) | async-done | bytes 25165840 | tf_op jit(solution)/shard_map/psum | solution.py:182
  1348.9 9.6 copy.116
  1358.5 5.7 copy.117
  1364.2 5.7 copy.118
  1369.9 204.1 %all-reduce.10.cloned.1.call-done = f32[2,512,3072]{2,1,0:T(8,128)} async-done(((f32[2,512,3072]{2,1,0:T(8,128)}), f32[2,512,3072]{2,1,0:T(8,128)}) %all-reduce.10.cloned.1.call-update) | async-done | bytes 12582928 | tf_op jit(solution)/shard_map/psum | solution.py:181
  1574.0 11.4 fusion.34
  1585.4 8.6 copy.226
  (288 shorter events, 225.0 us)
Async XLA Ops:
  7.2 501.7 %all-reduce.8.cloned.1.call-start = ((), (), s32[]{:S(2)}) async-start(), calls=%async_computation | async-start | bytes 25165824 | tf_op jit(solution)/shard_map/psum | solution.py:135
  7.4 55.0 %copy-start.10 = (pred[512,512]{0,1:T(8,128)(4,1)}, pred[512,512]{0,1:T(8,128)(4,1)S(1)}, u32[]{:S(2)}) copy-start(pred[512,512]{0,1:T(8,128)(4,1)S(1)} %iota_compare_fusion) | copy-start | bytes 786436
  21.0 22.1 %copy-start.8 = (f32[2,512,2,128]{1,3,2,0:T(8,128)}, f32[2,512,2,128]{1,3,2,0:T(8,128)S(1)}, u32[]{:S(2)}) copy-start(f32[2,512,2,128]{1,3,2,0:T(8,128)S(1)} %get-tuple-element.577) | copy-start | bytes 3145732
  21.0 22.1 %copy-start.47 = (f32[2,128]{1,0:T(2,128)S(1)}, f32[2,128]{1,0:T(2,128)}, u32[]{:S(2)}) copy-start(f32[2,128]{1,0:T(2,128)} %param.23) | copy-start | bytes 3076
  31.2 12.7 copy-start.45
  31.7 14.6 copy-start.24
  31.7 14.6 copy-start.26
  69.2 10.0 collective-permute-start.1
  73.0 11.7 collective-permute-start
  101.1 8.6 collective-permute-start.1
  103.6 11.7 collective-permute-start
  116.4 23.9 %collective-permute-start.1 = (bf16[2,512,2,128]{3,1,2,0:T(8,128)(2,1)S(1)}, bf16[2,512,2,128]{3,1,2,0:T(8,128)(2,1)S(1)}, u32[]{:S(2)}, u32[]{:S(2)}) collective-permute-start(bf16[2,512,2,128]{3,1,2,0:T(8,128)(2,1)S(1)} %get-tuple-element.735), channel_id=1, source_target_pairs={{0,1},{1,2},{2,3},{3,4},{4,5},{5,6},{6,7},{7,0},{8,9},{9,10},{10,1... | collective-permute-start | bytes 1572872 | tf_op jit(solution)/shard_map/while/body/eval_jaxpr/ppermute | solution.py:120
  134.3 11.7 collective-permute-start
  147.1 17.1 %collective-permute-start.1 = (bf16[2,512,2,128]{3,1,2,0:T(8,128)(2,1)S(1)}, bf16[2,512,2,128]{3,1,2,0:T(8,128)(2,1)S(1)}, u32[]{:S(2)}, u32[]{:S(2)}) collective-permute-start(bf16[2,512,2,128]{3,1,2,0:T(8,128)(2,1)S(1)} %get-tuple-element.735), channel_id=1, source_target_pairs={{0,1},{1,2},{2,3},{3,4},{4,5},{5,6},{6,7},{7,0},{8,9},{9,10},{10,1... | collective-permute-start | bytes 1572872 | tf_op jit(solution)/shard_map/while/body/eval_jaxpr/ppermute | solution.py:120
  149.6 20.7 %collective-permute-start = (bf16[2,512,2,128]{3,1,2,0:T(8,128)(2,1)S(1)}, bf16[2,512,2,128]{3,1,2,0:T(8,128)(2,1)}, u32[]{:S(2)}, u32[]{:S(2)}) collective-permute-start(bf16[2,512,2,128]{3,1,2,0:T(8,128)(2,1)S(1)} %get-tuple-element.734), channel_id=1, source_target_pairs={{0,1},{1,2},{2,3},{3,4},{4,5},{5,6},{6,7},{7,0},{8,9},{9,10},{10,1... | collective-permute-start | bytes 1572872 | tf_op jit(solution)/shard_map/while/body/eval_jaxpr/ppermute | solution.py:120
  171.3 8.6 collective-permute-start.1
  173.8 11.7 collective-permute-start
  186.7 23.4 %collective-permute-start.1 = (bf16[2,512,2,128]{3,1,2,0:T(8,128)(2,1)S(1)}, bf16[2,512,2,128]{3,1,2,0:T(8,128)(2,1)S(1)}, u32[]{:S(2)}, u32[]{:S(2)}) collective-permute-start(bf16[2,512,2,128]{3,1,2,0:T(8,128)(2,1)S(1)} %get-tuple-element.735), channel_id=1, source_target_pairs={{0,1},{1,2},{2,3},{3,4},{4,5},{5,6},{6,7},{7,0},{8,9},{9,10},{10,1... | collective-permute-start | bytes 1572872 | tf_op jit(solution)/shard_map/while/body/eval_jaxpr/ppermute | solution.py:120
  199.9 16.3 %collective-permute-start = (bf16[2,512,2,128]{3,1,2,0:T(8,128)(2,1)S(1)}, bf16[2,512,2,128]{3,1,2,0:T(8,128)(2,1)}, u32[]{:S(2)}, u32[]{:S(2)}) collective-permute-start(bf16[2,512,2,128]{3,1,2,0:T(8,128)(2,1)S(1)} %get-tuple-element.734), channel_id=1, source_target_pairs={{0,1},{1,2},{2,3},{3,4},{4,5},{5,6},{6,7},{7,0},{8,9},{9,10},{10,1... | collective-permute-start | bytes 1572872 | tf_op jit(solution)/shard_map/while/body/eval_jaxpr/ppermute | solution.py:120
  217.3 16.8 %collective-permute-start.1 = (bf16[2,512,2,128]{3,1,2,0:T(8,128)(2,1)S(1)}, bf16[2,512,2,128]{3,1,2,0:T(8,128)(2,1)S(1)}, u32[]{:S(2)}, u32[]{:S(2)}) collective-permute-start(bf16[2,512,2,128]{3,1,2,0:T(8,128)(2,1)S(1)} %get-tuple-element.735), channel_id=1, source_target_pairs={{0,1},{1,2},{2,3},{3,4},{4,5},{5,6},{6,7},{7,0},{8,9},{9,10},{10,1... | collective-permute-start | bytes 1572872 | tf_op jit(solution)/shard_map/while/body/eval_jaxpr/ppermute | solution.py:120
  219.8 20.4 %collective-permute-start = (bf16[2,512,2,128]{3,1,2,0:T(8,128)(2,1)S(1)}, bf16[2,512,2,128]{3,1,2,0:T(8,128)(2,1)}, u32[]{:S(2)}, u32[]{:S(2)}) collective-permute-start(bf16[2,512,2,128]{3,1,2,0:T(8,128)(2,1)S(1)} %get-tuple-element.734), channel_id=1, source_target_pairs={{0,1},{1,2},{2,3},{3,4},{4,5},{5,6},{6,7},{7,0},{8,9},{9,10},{10,1... | collective-permute-start | bytes 1572872 | tf_op jit(solution)/shard_map/while/body/eval_jaxpr/ppermute | solution.py:120
  241.2 13.4 copy-start.16
  254.7 1094.2 %all-reduce.12.cloned.1.call-start = ((), (), s32[]{:S(2)}) async-start(), calls=%async_computation.2 | async-start | bytes 50331648 | tf_op jit(solution)/shard_map/psum | solution.py:182
  258.7 255.8 %copy-start.43 = (f32[3072]{0:T(1024)S(1)}, f32[3072]{0:T(1024)}, u32[]{:S(2)}) copy-start(f32[3072]{0:T(1024)} %param.24) | copy-start | bytes 36868
  508.9 8.2 copy-start.4
  517.1 17.9 %slice-start.6 = ((s8[4718592]{0:T(1024)(128)(4,1)}), s8[4194304]{0:T(1024)(128)(4,1)S(1)}, s32[]{:S(2)}) async-start(s8[4718592]{0:T(1024)(128)(4,1)} %bitcast.206), calls=%async_computation.9 | async-start | bytes 8388608
  524.2 10.7 copy-start.33
  524.3 10.7 slice-start.7
  572.3 37.1 %collective-permute-start.5 = (f32[2,2,512,128]{3,2,1,0:T(8,128)}, f32[2,2,512,128]{3,2,1,0:T(8,128)S(1)}, u32[]{:S(2)}, u32[]{:S(2)}) collective-permute-start(f32[2,2,512,128]{3,2,1,0:T(8,128)} %get-tuple-element.767), channel_id=1, source_target_pairs={{0,1},{1,2},{2,3},{3,4},{4,5},{5,6},{6,7},{7,0},{8,9},{9,10},{10,1... | collective-permute-start | bytes 3145736 | tf_op jit(solution)/shard_map/while/body/eval_jaxpr/ppermute | solution.py:153
  574.3 35.0 %collective-permute-start.4 = (f32[2,2,512,128]{3,2,1,0:T(8,128)}, f32[2,2,512,128]{3,2,1,0:T(8,128)}, u32[]{:S(2)}, u32[]{:S(2)}) collective-permute-start(f32[2,2,512,128]{3,2,1,0:T(8,128)} %get-tuple-element.766), channel_id=1, source_target_pairs={{0,1},{1,2},{2,3},{3,4},{4,5},{5,6},{6,7},{7,0},{8,9},{9,10},{10,1... | collective-permute-start | bytes 3145736 | tf_op jit(solution)/shard_map/while/body/eval_jaxpr/ppermute | solution.py:153
  574.4 28.5 %collective-permute-start.3 = (bf16[2,512,2,128]{3,1,2,0:T(8,128)(2,1)}, bf16[2,512,2,128]{3,1,2,0:T(8,128)(2,1)}, u32[]{:S(2)}, u32[]{:S(2)}) collective-permute-start(bf16[2,512,2,128]{3,1,2,0:T(8,128)(2,1)} %get-tuple-element.765), channel_id=1, source_target_pairs={{0,1},{1,2},{2,3},{3,4},{4,5},{5,6},{6,7},{7,0},{8,9},{9,10},{10,1... | collective-permute-start | bytes 1572872 | tf_op jit(solution)/shard_map/while/body/eval_jaxpr/ppermute | solution.py:153
  575.9 32.6 %collective-permute-start.2 = (bf16[2,512,2,128]{3,1,2,0:T(8,128)(2,1)}, bf16[2,512,2,128]{3,1,2,0:T(8,128)(2,1)S(1)}, u32[]{:S(2)}, u32[]{:S(2)}) collective-permute-start(bf16[2,512,2,128]{3,1,2,0:T(8,128)(2,1)} %get-tuple-element.764), channel_id=1, source_target_pairs={{0,1},{1,2},{2,3},{3,4},{4,5},{5,6},{6,7},{7,0},{8,9},{9,10},{10,1... | collective-permute-start | bytes 1572872 | tf_op jit(solution)/shard_map/while/body/eval_jaxpr/ppermute | solution.py:153
  641.0 37.5 %collective-permute-start.5 = (f32[2,2,512,128]{3,2,1,0:T(8,128)}, f32[2,2,512,128]{3,2,1,0:T(8,128)S(1)}, u32[]{:S(2)}, u32[]{:S(2)}) collective-permute-start(f32[2,2,512,128]{3,2,1,0:T(8,128)} %get-tuple-element.767), channel_id=1, source_target_pairs={{0,1},{1,2},{2,3},{3,4},{4,5},{5,6},{6,7},{7,0},{8,9},{9,10},{10,1... | collective-permute-start | bytes 3145736 | tf_op jit(solution)/shard_map/while/body/eval_jaxpr/ppermute | solution.py:153
  643.5 35.0 %collective-permute-start.4 = (f32[2,2,512,128]{3,2,1,0:T(8,128)}, f32[2,2,512,128]{3,2,1,0:T(8,128)}, u32[]{:S(2)}, u32[]{:S(2)}) collective-permute-start(f32[2,2,512,128]{3,2,1,0:T(8,128)} %get-tuple-element.766), channel_id=1, source_target_pairs={{0,1},{1,2},{2,3},{3,4},{4,5},{5,6},{6,7},{7,0},{8,9},{9,10},{10,1... | collective-permute-start | bytes 3145736 | tf_op jit(solution)/shard_map/while/body/eval_jaxpr/ppermute | solution.py:153
  643.5 28.6 %collective-permute-start.3 = (bf16[2,512,2,128]{3,1,2,0:T(8,128)(2,1)}, bf16[2,512,2,128]{3,1,2,0:T(8,128)(2,1)}, u32[]{:S(2)}, u32[]{:S(2)}) collective-permute-start(bf16[2,512,2,128]{3,1,2,0:T(8,128)(2,1)} %get-tuple-element.765), channel_id=1, source_target_pairs={{0,1},{1,2},{2,3},{3,4},{4,5},{5,6},{6,7},{7,0},{8,9},{9,10},{10,1... | collective-permute-start | bytes 1572872 | tf_op jit(solution)/shard_map/while/body/eval_jaxpr/ppermute | solution.py:153
  645.1 32.6 %collective-permute-start.2 = (bf16[2,512,2,128]{3,1,2,0:T(8,128)(2,1)}, bf16[2,512,2,128]{3,1,2,0:T(8,128)(2,1)S(1)}, u32[]{:S(2)}, u32[]{:S(2)}) collective-permute-start(bf16[2,512,2,128]{3,1,2,0:T(8,128)(2,1)} %get-tuple-element.764), channel_id=1, source_target_pairs={{0,1},{1,2},{2,3},{3,4},{4,5},{5,6},{6,7},{7,0},{8,9},{9,10},{10,1... | collective-permute-start | bytes 1572872 | tf_op jit(solution)/shard_map/while/body/eval_jaxpr/ppermute | solution.py:153
  681.8 65.9 %collective-permute-start.5 = (f32[2,2,512,128]{3,2,1,0:T(8,128)}, f32[2,2,512,128]{3,2,1,0:T(8,128)S(1)}, u32[]{:S(2)}, u32[]{:S(2)}) collective-permute-start(f32[2,2,512,128]{3,2,1,0:T(8,128)} %get-tuple-element.767), channel_id=1, source_target_pairs={{0,1},{1,2},{2,3},{3,4},{4,5},{5,6},{6,7},{7,0},{8,9},{9,10},{10,1... | collective-permute-start | bytes 3145736 | tf_op jit(solution)/shard_map/while/body/eval_jaxpr/ppermute | solution.py:153
  712.7 35.0 %collective-permute-start.4 = (f32[2,2,512,128]{3,2,1,0:T(8,128)}, f32[2,2,512,128]{3,2,1,0:T(8,128)}, u32[]{:S(2)}, u32[]{:S(2)}) collective-permute-start(f32[2,2,512,128]{3,2,1,0:T(8,128)} %get-tuple-element.766), channel_id=1, source_target_pairs={{0,1},{1,2},{2,3},{3,4},{4,5},{5,6},{6,7},{7,0},{8,9},{9,10},{10,1... | collective-permute-start | bytes 3145736 | tf_op jit(solution)/shard_map/while/body/eval_jaxpr/ppermute | solution.py:153
  712.7 28.6 %collective-permute-start.3 = (bf16[2,512,2,128]{3,1,2,0:T(8,128)(2,1)}, bf16[2,512,2,128]{3,1,2,0:T(8,128)(2,1)}, u32[]{:S(2)}, u32[]{:S(2)}) collective-permute-start(bf16[2,512,2,128]{3,1,2,0:T(8,128)(2,1)} %get-tuple-element.765), channel_id=1, source_target_pairs={{0,1},{1,2},{2,3},{3,4},{4,5},{5,6},{6,7},{7,0},{8,9},{9,10},{10,1... | collective-permute-start | bytes 1572872 | tf_op jit(solution)/shard_map/while/body/eval_jaxpr/ppermute | solution.py:153
  714.3 32.6 %collective-permute-start.2 = (bf16[2,512,2,128]{3,1,2,0:T(8,128)(2,1)}, bf16[2,512,2,128]{3,1,2,0:T(8,128)(2,1)S(1)}, u32[]{:S(2)}, u32[]{:S(2)}) collective-permute-start(bf16[2,512,2,128]{3,1,2,0:T(8,128)(2,1)} %get-tuple-element.764), channel_id=1, source_target_pairs={{0,1},{1,2},{2,3},{3,4},{4,5},{5,6},{6,7},{7,0},{8,9},{9,10},{10,1... | collective-permute-start | bytes 1572872 | tf_op jit(solution)/shard_map/while/body/eval_jaxpr/ppermute | solution.py:153
  751.0 53.8 %collective-permute-start.5 = (f32[2,2,512,128]{3,2,1,0:T(8,128)}, f32[2,2,512,128]{3,2,1,0:T(8,128)S(1)}, u32[]{:S(2)}, u32[]{:S(2)}) collective-permute-start(f32[2,2,512,128]{3,2,1,0:T(8,128)} %get-tuple-element.767), channel_id=1, source_target_pairs={{0,1},{1,2},{2,3},{3,4},{4,5},{5,6},{6,7},{7,0},{8,9},{9,10},{10,1... | collective-permute-start | bytes 3145736 | tf_op jit(solution)/shard_map/while/body/eval_jaxpr/ppermute | solution.py:153
  753.5 51.3 %collective-permute-start.4 = (f32[2,2,512,128]{3,2,1,0:T(8,128)}, f32[2,2,512,128]{3,2,1,0:T(8,128)}, u32[]{:S(2)}, u32[]{:S(2)}) collective-permute-start(f32[2,2,512,128]{3,2,1,0:T(8,128)} %get-tuple-element.766), channel_id=1, source_target_pairs={{0,1},{1,2},{2,3},{3,4},{4,5},{5,6},{6,7},{7,0},{8,9},{9,10},{10,1... | collective-permute-start | bytes 3145736 | tf_op jit(solution)/shard_map/while/body/eval_jaxpr/ppermute | solution.py:153
  781.0 17.3 %collective-permute-start.3 = (bf16[2,512,2,128]{3,1,2,0:T(8,128)(2,1)}, bf16[2,512,2,128]{3,1,2,0:T(8,128)(2,1)}, u32[]{:S(2)}, u32[]{:S(2)}) collective-permute-start(bf16[2,512,2,128]{3,1,2,0:T(8,128)(2,1)} %get-tuple-element.765), channel_id=1, source_target_pairs={{0,1},{1,2},{2,3},{3,4},{4,5},{5,6},{6,7},{7,0},{8,9},{9,10},{10,1... | collective-permute-start | bytes 1572872 | tf_op jit(solution)/shard_map/while/body/eval_jaxpr/ppermute | solution.py:153
  783.5 20.5 %collective-permute-start.2 = (bf16[2,512,2,128]{3,1,2,0:T(8,128)(2,1)}, bf16[2,512,2,128]{3,1,2,0:T(8,128)(2,1)S(1)}, u32[]{:S(2)}, u32[]{:S(2)}) collective-permute-start(bf16[2,512,2,128]{3,1,2,0:T(8,128)(2,1)} %get-tuple-element.764), channel_id=1, source_target_pairs={{0,1},{1,2},{2,3},{3,4},{4,5},{5,6},{6,7},{7,0},{8,9},{9,10},{10,1... | collective-permute-start | bytes 1572872 | tf_op jit(solution)/shard_map/while/body/eval_jaxpr/ppermute | solution.py:153
  808.1 57.2 %collective-permute-start.5 = (f32[2,2,512,128]{3,2,1,0:T(8,128)}, f32[2,2,512,128]{3,2,1,0:T(8,128)S(1)}, u32[]{:S(2)}, u32[]{:S(2)}) collective-permute-start(f32[2,2,512,128]{3,2,1,0:T(8,128)} %get-tuple-element.767), channel_id=1, source_target_pairs={{0,1},{1,2},{2,3},{3,4},{4,5},{5,6},{6,7},{7,0},{8,9},{9,10},{10,1... | collective-permute-start | bytes 3145736 | tf_op jit(solution)/shard_map/while/body/eval_jaxpr/ppermute | solution.py:153
  810.6 54.7 %collective-permute-start.4 = (f32[2,2,512,128]{3,2,1,0:T(8,128)}, f32[2,2,512,128]{3,2,1,0:T(8,128)}, u32[]{:S(2)}, u32[]{:S(2)}) collective-permute-start(f32[2,2,512,128]{3,2,1,0:T(8,128)} %get-tuple-element.766), channel_id=1, source_target_pairs={{0,1},{1,2},{2,3},{3,4},{4,5},{5,6},{6,7},{7,0},{8,9},{9,10},{10,1... | collective-permute-start | bytes 3145736 | tf_op jit(solution)/shard_map/while/body/eval_jaxpr/ppermute | solution.py:153
  821.8 37.0 %collective-permute-start.3 = (bf16[2,512,2,128]{3,1,2,0:T(8,128)(2,1)}, bf16[2,512,2,128]{3,1,2,0:T(8,128)(2,1)}, u32[]{:S(2)}, u32[]{:S(2)}) collective-permute-start(bf16[2,512,2,128]{3,1,2,0:T(8,128)(2,1)} %get-tuple-element.765), channel_id=1, source_target_pairs={{0,1},{1,2},{2,3},{3,4},{4,5},{5,6},{6,7},{7,0},{8,9},{9,10},{10,1... | collective-permute-start | bytes 1572872 | tf_op jit(solution)/shard_map/while/body/eval_jaxpr/ppermute | solution.py:153
  852.7 11.7 collective-permute-start.2
  868.6 59.1 %collective-permute-start.5 = (f32[2,2,512,128]{3,2,1,0:T(8,128)}, f32[2,2,512,128]{3,2,1,0:T(8,128)S(1)}, u32[]{:S(2)}, u32[]{:S(2)}) collective-permute-start(f32[2,2,512,128]{3,2,1,0:T(8,128)} %get-tuple-element.767), channel_id=1, source_target_pairs={{0,1},{1,2},{2,3},{3,4},{4,5},{5,6},{6,7},{7,0},{8,9},{9,10},{10,1... | collective-permute-start | bytes 3145736 | tf_op jit(solution)/shard_map/while/body/eval_jaxpr/ppermute | solution.py:153
  871.1 56.6 %collective-permute-start.4 = (f32[2,2,512,128]{3,2,1,0:T(8,128)}, f32[2,2,512,128]{3,2,1,0:T(8,128)}, u32[]{:S(2)}, u32[]{:S(2)}) collective-permute-start(f32[2,2,512,128]{3,2,1,0:T(8,128)} %get-tuple-element.766), channel_id=1, source_target_pairs={{0,1},{1,2},{2,3},{3,4},{4,5},{5,6},{6,7},{7,0},{8,9},{9,10},{10,1... | collective-permute-start | bytes 3145736 | tf_op jit(solution)/shard_map/while/body/eval_jaxpr/ppermute | solution.py:153
  891.1 29.7 %collective-permute-start.3 = (bf16[2,512,2,128]{3,1,2,0:T(8,128)(2,1)}, bf16[2,512,2,128]{3,1,2,0:T(8,128)(2,1)}, u32[]{:S(2)}, u32[]{:S(2)}) collective-permute-start(bf16[2,512,2,128]{3,1,2,0:T(8,128)(2,1)} %get-tuple-element.765), channel_id=1, source_target_pairs={{0,1},{1,2},{2,3},{3,4},{4,5},{5,6},{6,7},{7,0},{8,9},{9,10},{10,1... | collective-permute-start | bytes 1572872 | tf_op jit(solution)/shard_map/while/body/eval_jaxpr/ppermute | solution.py:153
  893.6 33.3 %collective-permute-start.2 = (bf16[2,512,2,128]{3,1,2,0:T(8,128)(2,1)}, bf16[2,512,2,128]{3,1,2,0:T(8,128)(2,1)S(1)}, u32[]{:S(2)}, u32[]{:S(2)}) collective-permute-start(bf16[2,512,2,128]{3,1,2,0:T(8,128)(2,1)} %get-tuple-element.764), channel_id=1, source_target_pairs={{0,1},{1,2},{2,3},{3,4},{4,5},{5,6},{6,7},{7,0},{8,9},{9,10},{10,1... | collective-permute-start | bytes 1572872 | tf_op jit(solution)/shard_map/while/body/eval_jaxpr/ppermute | solution.py:153
  931.0 40.7 %collective-permute-start.5 = (f32[2,2,512,128]{3,2,1,0:T(8,128)}, f32[2,2,512,128]{3,2,1,0:T(8,128)S(1)}, u32[]{:S(2)}, u32[]{:S(2)}) collective-permute-start(f32[2,2,512,128]{3,2,1,0:T(8,128)} %get-tuple-element.767), channel_id=1, source_target_pairs={{0,1},{1,2},{2,3},{3,4},{4,5},{5,6},{6,7},{7,0},{8,9},{9,10},{10,1... | collective-permute-start | bytes 3145736 | tf_op jit(solution)/shard_map/while/body/eval_jaxpr/ppermute | solution.py:153
  933.5 38.2 %collective-permute-start.4 = (f32[2,2,512,128]{3,2,1,0:T(8,128)}, f32[2,2,512,128]{3,2,1,0:T(8,128)}, u32[]{:S(2)}, u32[]{:S(2)}) collective-permute-start(f32[2,2,512,128]{3,2,1,0:T(8,128)} %get-tuple-element.766), channel_id=1, source_target_pairs={{0,1},{1,2},{2,3},{3,4},{4,5},{5,6},{6,7},{7,0},{8,9},{9,10},{10,1... | collective-permute-start | bytes 3145736 | tf_op jit(solution)/shard_map/while/body/eval_jaxpr/ppermute | solution.py:153
  947.8 17.3 %collective-permute-start.3 = (bf16[2,512,2,128]{3,1,2,0:T(8,128)(2,1)}, bf16[2,512,2,128]{3,1,2,0:T(8,128)(2,1)}, u32[]{:S(2)}, u32[]{:S(2)}) collective-permute-start(bf16[2,512,2,128]{3,1,2,0:T(8,128)(2,1)} %get-tuple-element.765), channel_id=1, source_target_pairs={{0,1},{1,2},{2,3},{3,4},{4,5},{5,6},{6,7},{7,0},{8,9},{9,10},{10,1... | collective-permute-start | bytes 1572872 | tf_op jit(solution)/shard_map/while/body/eval_jaxpr/ppermute | solution.py:153
  950.3 20.5 %collective-permute-start.2 = (bf16[2,512,2,128]{3,1,2,0:T(8,128)(2,1)}, bf16[2,512,2,128]{3,1,2,0:T(8,128)(2,1)S(1)}, u32[]{:S(2)}, u32[]{:S(2)}) collective-permute-start(bf16[2,512,2,128]{3,1,2,0:T(8,128)(2,1)} %get-tuple-element.764), channel_id=1, source_target_pairs={{0,1},{1,2},{2,3},{3,4},{4,5},{5,6},{6,7},{7,0},{8,9},{9,10},{10,1... | collective-permute-start | bytes 1572872 | tf_op jit(solution)/shard_map/while/body/eval_jaxpr/ppermute | solution.py:153
  974.9 41.8 %copy-start.25 = (f32[512,64]{0,1:T(8,128)S(1)}, f32[512,64]{0,1:T(8,128)}, u32[]{:S(2)}) copy-start(f32[512,64]{0,1:T(8,128)} %copy-done.24) | copy-start | bytes 393220
  974.9 41.8 %copy-start.27 = (f32[512,64]{0,1:T(8,128)S(1)}, f32[512,64]{0,1:T(8,128)}, u32[]{:S(2)}) copy-start(f32[512,64]{0,1:T(8,128)} %copy-done.26) | copy-start | bytes 393220
  979.6 42.8 %collective-permute-start.7 = (bf16[2,2,512,128]{3,2,1,0:T(8,128)(2,1)}, bf16[2,2,512,128]{3,2,1,0:T(8,128)(2,1)}, u32[]{:S(2)}, u32[]{:S(2)}) collective-permute-start(bf16[2,2,512,128]{3,2,1,0:T(8,128)(2,1)} %convert.30), channel_id=1, source_target_pairs={{0,1},{1,2},{2,3},{3,4},{4,5},{5,6},{6,7},{7,0},{8,9},{9,10},{10,1... | collective-permute-start | bytes 1572872 | tf_op jit(solution)/shard_map/ppermute | solution.py:166
  1003.1 23.9 %collective-permute-start.6 = (f32[2,2,512,128]{2,3,1,0:T(8,128)}, f32[2,2,512,128]{2,3,1,0:T(8,128)}, u32[]{:S(2)}, u32[]{:S(2)}) collective-permute-start(f32[2,2,512,128]{2,3,1,0:T(8,128)} %copy.111), channel_id=1, source_target_pairs={{0,1},{1,2},{2,3},{3,4},{4,5},{5,6},{6,7},{7,0},{8,9},{9,10},{10,1... | collective-permute-start | bytes 3145736 | tf_op jit(solution)/shard_map/ppermute | solution.py:166
  1037.8 9.6 copy-start.28
  1037.8 9.6 slice-start.2
  1054.9 519.1 %all-reduce.10.cloned.1.call-start = ((), (), s32[]{:S(2)}) async-start(), calls=%async_computation.1 | async-start | bytes 25165824 | tf_op jit(solution)/shard_map/psum | solution.py:181
  1062.8 10.8 copy-start.32
  (40 other events, 168.7 us)
Sparse Core Ops, SparseCore 0:
  254.8 254.1 all-reduce.7
  1055.1 293.7 all-reduce.11
  1351.4 222.5 all-reduce.9
where the time goes:
time: 1610 us; the launch traced here: 1600 us
  waiting for transfers between devices  843 us (52%)
  starting transfers between devices  324 us (20%)
  matrix products  161 us (10%)
  local copies, waits for them, and re-layouts  107 us (7%)
  blocking collectives  79.8 us (5%)
  other arithmetic  71.7 us (4%)
    psum x1, waiting for transfers between devices, local_run(): lax.psum(jnp.einsum('blhe,hed->bld', attn_out, w_o, preferred_element_typ...  249 us
    psum x1, waiting for transfers between devices, local_run(): grad_x = (grad_f + lax.psum(grad_x_part, 'tp')).astype(jnp.bfloat16)  204 us
    ppermute x28, starting transfers between devices, bwd_step(): lax.ppermute((k_cur, v_cur, dk_cur, dv_cur), 'cp', perm_next)  200 us
    psum x1, waiting for transfers between devices, local_run(): lax.psum((grad_w_q, grad_w_k, grad_w_v, grad_w_o, grad_q_norm, grad_k_nor...  198 us
    ppermute x28, waiting for transfers between devices, bwd_step(): lax.ppermute((k_cur, v_cur, dk_cur, dv_cur), 'cp', perm_next)  132 us
    ppermute x14, starting transfers between devices, fwd_step(): k_cur, v_cur = lax.ppermute((k_cur, v_cur), 'cp', perm_next)  89.7 us
    psum x1, blocking collectives, local_run(): lax.psum((grad_w_q, grad_w_k, grad_w_v, grad_w_o, grad_q_norm, grad_k_nor...  61.8 us
    ppermute x14, waiting for transfers between devices, fwd_step(): k_cur, v_cur = lax.ppermute((k_cur, v_cur), 'cp', perm_next)  59.5 us
  transfers between devices with their start and end apart: 47, of which 27 were waited for; matrix products, arithmetic and copies ran while one was open for 6% of the time, Pallas kernels for 0%

commit v1 on v0

v1 whole, which is shorter than its diff:
```python
import functools

import jax
import jax.numpy as jnp
from jax import lax
from jax.experimental import pallas as pl
from jax.experimental.pallas import tpu as pltpu
from jax.sharding import PartitionSpec as P

ROPE_THETA = 500000.0
NORM_EPS = 1e-6
MASK_VALUE = -1e30
LOG2E = 1.4426950408889634
NT = (((1,), (1,)), ((), ()))
NN = (((1,), (0,)), ((), ()))
TN = (((0,), (0,)), ((), ()))


def rope_tables(start_pos, seq_rows, head_dim):
    half_dim = head_dim // 2
    inv_freq = ROPE_THETA ** (-2.0 * jnp.arange(half_dim, dtype=jnp.float32) / head_dim)
    positions = (start_pos + jnp.arange(seq_rows)).astype(jnp.float32)
    angles = positions[:, None] * inv_freq[None, :]
    return jnp.cos(angles), jnp.sin(angles)


def apply_rope(values, cos_tab, sin_tab):
    half_dim = values.shape[-1] // 2
    low_half = values[..., :half_dim]
    high_half = values[..., half_dim:]
    cos_rows = cos_tab[:, None, :]
    sin_rows = sin_tab[:, None, :]
    return jnp.concatenate([low_half * cos_rows - high_half * sin_rows, high_half * cos_rows + low_half * sin_rows], axis=-1)


def rope_back(grad_in, cos_tab, sin_tab):
    return apply_rope(grad_in, cos_tab, -sin_tab)


def dot32(lhs, rhs, dims):
    return lax.dot_general(lhs, rhs, dims, preferred_element_type=jnp.float32)


def attend_kernel(n_group, score_scale, q_ref, k_ref, v_ref, o_ref, lse_ref, acc_ref, max_ref):
    block_len = q_ref.shape[0]
    dim = k_ref.shape[2]
    me = lax.axis_index("cp")
    to_log2 = score_scale * LOG2E
    n_rep = block_len // dim

    def one_block(blk, first):
        k_blk = k_ref[blk]
        v_ext = jnp.concatenate([v_ref[blk], jnp.ones((block_len, dim), jnp.bfloat16)], axis=1)
        for grp in range(n_group):
            q_grp = q_ref[:, grp * dim:(grp + 1) * dim]
            scores = dot32(q_grp, k_blk, NT) * to_log2
            if first:
                rows = lax.broadcasted_iota(jnp.int32, scores.shape, 0)
                cols = lax.broadcasted_iota(jnp.int32, scores.shape, 1)
                scores = jnp.where(rows >= cols, scores, MASK_VALUE)
                new_max = jnp.broadcast_to(jnp.max(scores, axis=1, keepdims=True), (block_len, dim))
                prob = jnp.exp2(scores - jnp.concatenate([new_max] * n_rep, axis=1))
                acc_ref[grp] = dot32(prob.astype(jnp.bfloat16), v_ext, NN)
            else:
                old_max = max_ref[grp]
                new_max = jnp.maximum(old_max, jnp.broadcast_to(jnp.max(scores, axis=1, keepdims=True), (block_len, dim)))
                prob = jnp.exp2(scores - jnp.concatenate([new_max] * n_rep, axis=1))
                rescale = jnp.exp2(old_max - new_max)
                acc_ref[grp] = (acc_ref[grp] * jnp.concatenate([rescale, rescale], axis=1)
                                + dot32(prob.astype(jnp.bfloat16), v_ext, NN))
            max_ref[grp] = new_max

    one_block(me, True)

    def step(blk, carry):
        one_block(blk, False)
        return carry

    lax.fori_loop(0, me, step, 0)
    for grp in range(n_group):
        row_sum = acc_ref[grp, :, dim:]
        o_ref[:, grp * dim:(grp + 1) * dim] = (acc_ref[grp, :, :dim] / row_sum).astype(jnp.bfloat16)
        lse = jnp.transpose(max_ref[grp] + jnp.log2(row_sum))
        lse_ref[0, grp:grp + 1, :] = lse[0:1, :]


def attend_back_kernel(n_group, score_scale, q_ref, do_ref, o_ref, lse_ref, k_ref, v_ref, dq_ref, dk_ref, dv_ref, delta_ref):
    block_len = q_ref.shape[0]
    dim = k_ref.shape[2]
    n_blocks = k_ref.shape[0]
    me = lax.axis_index("cp")
    to_log2 = score_scale * LOG2E
    for grp in range(n_group):
        lanes = slice(grp * dim, (grp + 1) * dim)
        prod = do_ref[:, lanes].astype(jnp.float32) * o_ref[:, lanes].astype(jnp.float32)
        delta_ref[grp:grp + 1, :] = jnp.sum(jnp.transpose(prod), axis=0, keepdims=True)

    def one_block(blk, first):
        k_blk = k_ref[blk]
        v_blk = v_ref[blk]
        dk_sum = None
        dv_sum = None
        for grp in range(n_group):
            lanes = slice(grp * dim, (grp + 1) * dim)
            q_grp = q_ref[:, lanes]
            do_grp = do_ref[:, lanes]
            scores = dot32(k_blk, q_grp, NT) * to_log2
            if first:
                rows = lax.broadcasted_iota(jnp.int32, scores.shape, 0)
                cols = lax.broadcasted_iota(jnp.int32, scores.shape, 1)
                scores = jnp.where(cols >= rows, scores, MASK_VALUE)
            prob = jnp.exp2(scores - lse_ref[0, grp:grp + 1, :])
            grad_p = dot32(v_blk, do_grp, NT)
            grad_s = (prob * (grad_p - delta_ref[grp:grp + 1, :])).astype(jnp.bfloat16)
            dv_part = dot32(prob.astype(jnp.bfloat16), do_grp, NN)
            dk_part = dot32(grad_s, q_grp, NN)
            dq_part = dot32(grad_s, k_blk, TN)
            dv_sum = dv_part if dv_sum is None else dv_sum + dv_part
            dk_sum = dk_part if dk_sum is None else dk_sum + dk_part
            if first:
                dq_ref[:, lanes] = dq_part
            else:
                dq_ref[:, lanes] += dq_part
        dk_ref[blk] = dk_sum * score_scale
        dv_ref[blk] = dv_sum

    one_block(me, True)

    def step(blk, carry):
        one_block(blk, False)
        return carry

    lax.fori_loop(0, me, step, 0)
    dq_ref[...] = dq_ref[...] * score_scale

    def clear(blk, carry):
        dk_ref[blk] = jnp.zeros((block_len, dim), jnp.float32)
        dv_ref[blk] = jnp.zeros((block_len, dim), jnp.float32)
        return carry

    lax.fori_loop(me + 1, n_blocks, clear, 0)


def attend(q_rot, kv_all, kv_loc, n_group, dim, score_scale):
    block_len, q_cols = q_rot.shape
    n_blocks = kv_all.shape[0]
    wide = n_group * dim
    pairs = kv_loc * n_group * n_blocks * block_len * block_len
    return pl.pallas_call(
        functools.partial(attend_kernel, n_group, score_scale),
        grid=(kv_loc,),
        in_specs=[
            pl.BlockSpec((block_len, wide), lambda h: (0, h)),
            pl.BlockSpec((n_blocks, block_len, dim), lambda h: (0, 0, h)),
            pl.BlockSpec((n_blocks, block_len, dim), lambda h: (0, 0, kv_loc + h)),
        ],
        out_specs=[
            pl.BlockSpec((block_len, wide), lambda h: (0, h)),
            pl.BlockSpec((1, n_group, block_len), lambda h: (h, 0, 0)),
        ],
        out_shape=[
            jax.ShapeDtypeStruct((block_len, q_cols), jnp.bfloat16),
            jax.ShapeDtypeStruct((kv_loc, n_group, block_len), jnp.float32),
        ],
        scratch_shapes=[
            pltpu.VMEM((n_group, block_len, 2 * dim), jnp.float32),
            pltpu.VMEM((n_group, block_len, dim), jnp.float32),
        ],
        compiler_params=pltpu.CompilerParams(vmem_limit_bytes=40 * 1024 * 1024),
        cost_estimate=pl.CostEstimate(flops=8 * pairs * dim, bytes_accessed=2 * kv_all.size, transcendentals=pairs),
        name="attend",
    )(q_rot, kv_all, kv_all)


def attend_back(q_rot, grad_o, attn_out, lse, kv_all, kv_loc, n_group, dim, score_scale):
    block_len, q_cols = q_rot.shape
    n_blocks = kv_all.shape[0]
    wide = n_group * dim
    pairs = kv_loc * n_group * n_blocks * block_len * block_len
    q_spec = pl.BlockSpec((block_len, wide), lambda h: (0, h))
    k_spec = pl.BlockSpec((n_blocks, block_len, dim), lambda h: (0, 0, h))
    return pl.pallas_call(
        functools.partial(attend_back_kernel, n_group, score_scale),
        grid=(kv_loc,),
        in_specs=[
            q_spec, q_spec, q_spec,
            pl.BlockSpec((1, n_group, block_len), lambda h: (h, 0, 0)),
            k_spec,
            pl.BlockSpec((n_blocks, block_len, dim), lambda h: (0, 0, kv_loc + h)),
        ],
        out_specs=[q_spec, k_spec, k_spec],
        out_shape=[
            jax.ShapeDtypeStruct((block_len, q_cols), jnp.float32),
            jax.ShapeDtypeStruct((n_blocks, block_len, kv_loc * dim), jnp.float32),
            jax.ShapeDtypeStruct((n_blocks, block_len, kv_loc * dim), jnp.float32),
        ],
        scratch_shapes=[pltpu.VMEM((n_group, block_len), jnp.float32)],
        compiler_params=pltpu.CompilerParams(vmem_limit_bytes=48 * 1024 * 1024),
        cost_estimate=pl.CostEstimate(flops=20 * pairs * dim, bytes_accessed=4 * kv_all.size, transcendentals=pairs),
        name="attend_back",
    )(q_rot, grad_o, attn_out, lse, kv_all, kv_all)


def solution(mesh):
    tp_size = mesh.shape["tp"]
    cp_size = mesh.shape["cp"]
    tp_next = [(dev, (dev + 1) % tp_size) for dev in range(tp_size)]
    tp_prev = [(dev, (dev + tp_size - 1) % tp_size) for dev in range(tp_size)]
    swap_core = [(dev, dev ^ 1) for dev in range(cp_size)]
    act_spec = P("dp", "cp", None)
    col_spec = P(None, "tp", None)
    part_col = P("dp", "tp", None)
    in_specs = (act_spec, col_spec, col_spec, col_spec, P("tp", None, None), P("tp", None), P("tp", None), P(None), act_spec)
    out_specs = (act_spec, act_spec, part_col, part_col, part_col, P(("dp", "tp"), None, None), P(("dp", "tp"), None), P(("dp", "tp"), None), P("dp"))

    def gather_tp_rows(w_loc, core):
        half_rows = w_loc.shape[0] // 2
        quarter = half_rows // 2
        mine = lax.dynamic_slice_in_dim(w_loc, core * half_rows, half_rows, 0)
        lower = lax.ppermute(mine, "tp", tp_next)
        upper = lax.ppermute(mine, "tp", tp_prev)
        far_a = lax.ppermute(lower[:quarter], "tp", tp_next)
        far_b = lax.ppermute(upper[quarter:], "tp", tp_prev)
        out = []
        for got in (lower, upper, jnp.concatenate([far_a, far_b], axis=0)):
            other = lax.ppermute(got, "cp", swap_core)
            out.append(jnp.where(core == 0, jnp.concatenate([got, other], axis=0), jnp.concatenate([other, got], axis=0)))
        return out

    def local_run(x_in, w_q, w_k, w_v, w_o, q_norm_w, k_norm_w, post_norm_w, grad_y):
        n_batch, block_len, width = x_in.shape
        heads_loc = w_q.shape[1]
        kv_loc = w_k.shape[1]
        dim = w_q.shape[2]
        n_group = heads_loc // kv_loc
        q_cols = heads_loc * dim
        k_cols = kv_loc * dim
        q_width = q_cols * tp_size
        k_width = k_cols * tp_size
        score_scale = dim ** -0.5
        cp_index = lax.axis_index("cp")
        tp_index = lax.axis_index("tp")
        core = lax.rem(cp_index, 2)
        cos_tab, sin_tab = rope_tables(cp_index * block_len, block_len, dim)
        w_o2 = w_o.reshape(q_cols, width)
        wo_parts = [w_o2] + gather_tp_rows(w_o2, core)

        q_lin = jnp.einsum("bld,dhe->blhe", x_in, w_q, preferred_element_type=jnp.float32)
        k_lin = jnp.einsum("bld,dhe->blhe", x_in, w_k, preferred_element_type=jnp.float32)
        v_lin = jnp.einsum("bld,dhe->blhe", x_in, w_v, preferred_element_type=jnp.float32)
        sums = jnp.stack([jnp.sum(q_lin * q_lin, axis=(2, 3)), jnp.sum(k_lin * k_lin, axis=(2, 3))])
        sums = lax.psum(sums, "tp")
        q_inv = lax.rsqrt(sums[0] / q_width + NORM_EPS)[:, :, None, None]
        k_inv = lax.rsqrt(sums[1] / k_width + NORM_EPS)[:, :, None, None]
        q_hat = q_lin * q_inv
        k_hat = k_lin * k_inv
        k_rot = apply_rope(k_hat * k_norm_w, cos_tab, sin_tab).astype(jnp.bfloat16).reshape(n_batch, block_len, k_cols)
        v_val = v_lin.astype(jnp.bfloat16).reshape(n_batch, block_len, k_cols)
        q_rot = apply_rope(q_hat * q_norm_w, cos_tab, sin_tab).astype(jnp.bfloat16).reshape(n_batch, block_len, q_cols)
        kv_own = jnp.concatenate([k_rot, v_val], axis=2)
        kv_all = [lax.all_gather(kv_own[b], "cp") for b in range(n_batch)]

        y_list, gproj_list, o_list, lse_list, gpost_list = [], [], [], [], []
        for b in range(n_batch):
            attn_out, lse = attend(q_rot[b], kv_all[b], kv_loc, n_group, dim, score_scale)
            o_list.append(attn_out)
            lse_list.append(lse)
        for b in range(n_batch):
            o_all = lax.all_gather(o_list[b], "tp")
            proj = dot32(o_list[b], wo_parts[0], NN)
            for part, shift in ((1, tp_size - 1), (2, 1), (3, 2)):
                o_part = lax.dynamic_index_in_dim(o_all, lax.rem(tp_index + shift, tp_size), 0, keepdims=False)
                proj = proj + dot32(o_part, wo_parts[part], NN)
            post_inv = lax.rsqrt(jnp.mean(proj * proj, axis=-1, keepdims=True) + NORM_EPS)
            post_hat = proj * post_inv
            y_list.append((x_in[b] + post_hat * post_norm_w).astype(jnp.bfloat16))
            grad_f = grad_y[b].astype(jnp.float32)
            gpost_list.append(jnp.sum(grad_f * post_hat, axis=0))
            grad_hat = grad_f * post_norm_w
            gproj_list.append((post_inv * (grad_hat - post_hat * jnp.mean(grad_hat * post_hat, axis=-1, keepdims=True))).astype(jnp.bfloat16))
        y_out = jnp.stack(y_list)
        grad_post = gpost_list[0]
        for term in gpost_list[1:]:
            grad_post = grad_post + term

        gq_list, gk_list, gv_list, gqn, gkn = [], [], [], 0.0, 0.0
        dx_list = []
        for b in range(n_batch):
            grad_o = dot32(gproj_list[b], w_o2, NT).astype(jnp.bfloat16)
            dq_rot, dk_all, dv_all = attend_back(q_rot[b], grad_o, o_list[b], lse_list[b], kv_all[b], kv_loc, n_group, dim, score_scale)
            dkv = lax.psum_scatter(jnp.concatenate([dk_all, dv_all], axis=2), "cp", scatter_dimension=0, tiled=False)
            dk_rot = dkv[:, :k_cols].reshape(block_len, kv_loc, dim)
            grad_v16 = dkv[:, k_cols:].astype(jnp.bfloat16)
            grad_q = rope_back(dq_rot.reshape(block_len, heads_loc, dim), cos_tab, sin_tab)
            grad_k = rope_back(dk_rot, cos_tab, sin_tab)
            gqn = gqn + jnp.sum(grad_q * q_hat[b], axis=0)
            gkn = gkn + jnp.sum(grad_k * k_hat[b], axis=0)
            grad_q = grad_q * q_norm_w
            grad_k = grad_k * k_norm_w
            dots = lax.psum(jnp.stack([jnp.sum(grad_q * q_hat[b], axis=(1, 2)), jnp.sum(grad_k * k_hat[b], axis=(1, 2))]), "tp")
            grad_q16 = (q_inv[b] * (grad_q - q_hat[b] * (dots[0] / q_width)[:, None, None])).astype(jnp.bfloat16)
            grad_k16 = (k_inv[b] * (grad_k - k_hat[b] * (dots[1] / k_width)[:, None, None])).astype(jnp.bfloat16)
            grad_v16 = grad_v16.reshape(block_len, kv_loc, dim)
            dx_part = (jnp.einsum("lhe,dhe->ld", grad_q16, w_q, preferred_element_type=jnp.float32)
                       + jnp.einsum("lhe,dhe->ld", grad_k16, w_k, preferred_element_type=jnp.float32)
                       + jnp.einsum("lhe,dhe->ld", grad_v16, w_v, preferred_element_type=jnp.float32))
            dx_own = lax.psum_scatter(dx_part, "tp", scatter_dimension=0, tiled=True)
            rows = dx_own.shape[0]
            gy_own = lax.dynamic_slice_in_dim(grad_y[b], tp_index * rows, rows, 0).astype(jnp.float32)
            dx_list.append(lax.all_gather((gy_own + dx_own).astype(jnp.bfloat16), "tp", tiled=True))
            gq_list.append(grad_q16)
            gk_list.append(grad_k16)
            gv_list.append(grad_v16)
        grad_x = jnp.stack(dx_list)
        grad_w_o = lax.psum(jnp.einsum("ble,bld->ed", jnp.stack(o_list), jnp.stack(gproj_list), preferred_element_type=jnp.float32), "cp")
        grad_w_q = jnp.einsum("bld,blhe->dhe", x_in, jnp.stack(gq_list), preferred_element_type=jnp.float32)
        grad_w_k = jnp.einsum("bld,blhe->dhe", x_in, jnp.stack(gk_list), preferred_element_type=jnp.float32)
        grad_w_v = jnp.einsum("bld,blhe->dhe", x_in, jnp.stack(gv_list), preferred_element_type=jnp.float32)
        grad_w_q, grad_w_k, grad_w_v, gqn, gkn, grad_post = lax.psum((grad_w_q, grad_w_k, grad_w_v, gqn, gkn, grad_post), "cp")
        return (y_out, grad_x, grad_w_q, grad_w_k, grad_w_v, grad_w_o.reshape(heads_loc, dim, width), gqn, gkn, grad_post)

    return jax.shard_map(local_run, mesh=mesh, in_specs=in_specs, out_specs=out_specs, check_vma=False)
```

time: 1610 us -> 974 us (0.60)
  waiting for transfers between devices: 843 us -> 531 us
  starting transfers between devices: 324 us -> 19.7 us
  Pallas kernels: 0 us -> 44.1 us
  blocking collectives: 79.8 us -> 43.5 us
  local copies, waits for them, and re-layouts: 107 us -> 80.1 us
    psum x3 -> x1, waiting for transfers between devices: 652 us -> 228 us  [local_run(): lax.psum((grad_w_q, grad_w_k, grad_w_v, gqn, gkn, grad_post), 'cp')]
    ppermute x44 -> x7, starting transfers between devices: 323 us -> 19 us  [the longest x3 15.9 us: gather_tp_rows(): other = lax.ppermute(got, 'cp', swap_core)]
    reduce_scatter x0 -> x4, waiting for transfers between devices: none -> 164 us  [the longest x2 99.1 us: local_run(): lax.psum_scatter(jnp.concatenate([dk_all, dv_all], axis=2), 'cp', scatter...]
    ppermute x44 -> x7, waiting for transfers between devices: 192 us -> 45.1 us  [the longest x1 23.5 us: gather_tp_rows(): far_b = lax.ppermute(upper[quarter:], 'tp', tp_prev)]
    all_gather x0 -> x6, waiting for transfers between devices: none -> 92.1 us  [the longest x2 58.4 us: local_run(): lax.all_gather((gy_own + dx_own).astype(jnp.bfloat16), 'tp', tiled=True)]
    while x45 -> x0, local copies, waits for them, and re-layouts: 54.2 us -> none
    pallas_call x0 -> x4, Pallas kernels: none -> 44.1 us  [the longest x2 29.1 us: attend_back(): pl.pallas_call(functools.partial(attend_back_kernel, n_group, score_scale...]
    psum x3, blocking collectives: 79.8 us -> 43.5 us  [the longest x1 23.5 us: local_run(): lax.psum((grad_w_q, grad_w_k, grad_w_v, gqn, gkn, grad_post), 'cp')]
  transfers between devices with their start and end apart: 47 -> 18, of which waited for: 27 -> 12; matrix products, arithmetic and copies ran while one was open for 6% -> 17% of each run, Pallas kernels for 0% -> 3%
where the time goes in v1:
time: 974 us; the launch traced here: 966 us
  waiting for transfers between devices  531 us (55%)
  matrix products  154 us (16%)
  local copies, waits for them, and re-layouts  80.1 us (8%)
  other arithmetic  78.6 us (8%)
  Pallas kernels  44.1 us (5%)
  blocking collectives  43.5 us (4%)
  starting transfers between devices  19.7 us (2%)
  between operations  15.2 us (2%)
    psum x1, waiting for transfers between devices, local_run(): lax.psum((grad_w_q, grad_w_k, grad_w_v, gqn, gkn, grad_post), 'cp')  228 us
    reduce_scatter x2, waiting for transfers between devices, local_run(): lax.psum_scatter(jnp.concatenate([dk_all, dv_all], axis=2), 'cp', scatter...  99.1 us
    dot_general x10, matrix products, dot32(): return lax.dot_general(lhs, rhs, dims, preferred_element_type=jnp.float32)  83.2 us
    reduce_scatter x2, waiting for transfers between devices, local_run(): dx_own = lax.psum_scatter(dx_part, 'tp', scatter_dimension=0, tiled=True)  64.8 us
    all_gather x2, waiting for transfers between devices, local_run(): lax.all_gather((gy_own + dx_own).astype(jnp.bfloat16), 'tp', tiled=True)  58.4 us
    unnamed x118, local copies, waits for them, and re-layouts  42.8 us
    pallas_call x2, Pallas kernels, attend_back(): pl.pallas_call(functools.partial(attend_back_kernel, n_group, score_scale...  29.1 us
    psum x1, blocking collectives, local_run(): lax.psum((grad_w_q, grad_w_k, grad_w_v, gqn, gkn, grad_post), 'cp')  23.5 us
  transfers between devices with their start and end apart: 18, of which 12 were waited for; matrix products, arithmetic and copies ran while one was open for 17% of the time, Pallas kernels for 3%

profile of v1, /device:TPU:97, one launch (start us, length us, event | category | flops | bytes accessed | tf_op | source)
XLA Modules:
  0.0 965.9 jit_solution(3878849846270665475)
XLA Ops:
  7.3 3.6 copy.85
  10.9 3.9 copy.86
  14.8 6.1 multiply_reduce_fusion.3
  20.9 5.4 fusion.68
  28.4 8.8 multiply_reduce_fusion.2
  37.2 11.3 %psum.70 = f32[2,2,512]{2,1,0:T(2,128)S(1)} all-reduce(f32[2,2,512]{2,1,0:T(2,128)S(1)} %pad_maximum_fusion.12), channel_id=1, replica_groups=mesh['dp'=1,'tp'=4,'cp'=8] {'tp'}, use_global_device_ids=true, to_apply=%region_2.3 | all-reduce | flops 2048 | bytes 16384 | tf_op jit(solution)/shard_map/psum | solution.py:252
  58.9 3.2 constant_dynamic-slice_fusion
  66.9 22.3 %all-gather.9.cloned.1.call-done.k_ref.v_ref = bf16[8,512,512]{2,1,0:T(8,128)(2,1)} async-done(((bf16[1,512,512]{2,1,0:T(8,128)(2,1)}), bf16[8,512,512]{2,1,0:T(8,128)(2,1)}) %all-gather.9.cloned.1.call-update) | async-done | bytes 4194320 | tf_op jit(solution)/shard_map/all_gather | solution.py:261
  91.4 7.5 attend.2
  99.1 13.4 %collective-permute-done.2 = bf16[384,3072]{1,0:T(8,128)(2,1)} collective-permute-done((bf16[384,3072]{1,0:T(8,128)(2,1)}, bf16[384,3072]{1,0:T(8,128)(2,1)}, u32[]{:S(2)}, u32[]{:S(2)}) %collective-permute-start.2) | collective-permute-done | bytes 2359328 | tf_op jit(solution)/shard_map/ppermute | solution.py:221
  112.5 2.4 slice.195
  116.3 2.4 slice.194
  118.9 4.0 collective-permute-start.1
  123.0 23.5 %collective-permute-done.5 = bf16[192,3072]{1,0:T(8,128)(2,1)} collective-permute-done((bf16[192,3072]{1,0:T(8,128)(2,1)}, bf16[192,3072]{1,0:T(8,128)(2,1)}, u32[]{:S(2)}, u32[]{:S(2)}) %collective-permute-start.5) | collective-permute-done | bytes 1179680 | tf_op jit(solution)/shard_map/ppermute | solution.py:223
  146.5 8.2 collective-permute-done.4
  154.7 3.2 pad_maximum_fusion.4
  157.9 11.8 %collective-permute-start.6 = (bf16[384,3072]{1,0:T(8,128)(2,1)}, bf16[384,3072]{1,0:T(8,128)(2,1)}, u32[]{:S(2)}, u32[]{:S(2)}) collective-permute-start(bf16[384,3072]{1,0:T(8,128)(2,1)} %pad_maximum_fusion.4), channel_id=1, source_target_pairs={{0,1},{1,0},{2,3},{3,2},{4,5},{5,4},{6,7},{7,6},{8,9},{9,8},{10,11... | collective-permute-start | bytes 7077896 | tf_op jit(solution)/shard_map/ppermute | solution.py:226
  171.9 7.5 attend.3
  179.7 8.0 fusion.165
  187.7 5.9 fusion.166
  193.6 9.5 fusion.74
  203.1 7.3 fusion.84
  210.4 11.7 %multiply_reduce_fusion.1 = (f32[512]{0:T(512)S(1)}, f32[512,3072]{1,0:T(8,128)}) fusion(f32[512,3072]{1,0:T(8,128)} %fusion.84, bf16[384,3072]{1,0:T(8,128)(2,1)} %collective-permute-done.3, bf16[384,3072]{1,0:T(8,128)(2,1)} %collective-permute-done.2, pred[]{:T(512)S(6)} %eq.2, bf16[4,512,768]{2,1,0:T(8,128)(2,1)S(1)} %bitcast.325, s32[]{:T(128)S(6)} %select_n.40, ...), kind=kOutput, calls=%fused_computation.46 | convolution fusion | flops 2445016576 | bytes 30672900 | tf_op jit(solution)/shard_map/dot_general | solution.py:41
  222.0 11.4 %all-gather.19.cloned.1.call-done = bf16[2048,768]{1,0:T(8,128)(2,1)} async-done(((bf16[512,768]{1,0:T(8,128)(2,1)}), bf16[2048,768]{1,0:T(8,128)(2,1)}) %all-gather.19.cloned.1.call-update) | async-done | bytes 3145744 | tf_op jit(solution)/shard_map/all_gather | solution.py:269
  233.4 7.4 fusion.80
  240.8 9.3 fusion.73
  250.1 13.7 %multiply_reduce_fusion = (f32[512]{0:T(512)S(1)}, f32[512,3072]{1,0:T(8,128)}) fusion(f32[512,3072]{1,0:T(8,128)} %fusion.80, bf16[384,3072]{1,0:T(8,128)(2,1)} %collective-permute-done.3, bf16[384,3072]{1,0:T(8,128)(2,1)} %collective-permute-done.2, pred[]{:T(512)S(6)} %eq.2, bf16[4,512,768]{2,1,0:T(8,128)(2,1)S(1)} %bitcast.328, s32[]{:T(128)S(6)} %select_n.40, ...), kind=kOutput, calls=%fused_computation.44 | convolution fusion | flops 2445016576 | bytes 30672900 | tf_op jit(solution)/shard_map/dot_general | solution.py:41
  263.9 7.9 fusion.10
  271.7 12.3 %fusion.6 = (bf16[512,3072]{1,0:T(8,128)(2,1)}, bf16[1,512,3072]{2,1,0:T(8,128)(2,1)}, bf16[1,512,3072]{2,1,0:T(8,128)(2,1)}, bf16[512,3072]{1,0:T(8,128)(2,1)}) fusion(f32[512,3072]{1,0:T(8,128)} %get-tuple-element.141, f32[512]{0:T(512)S(1)} %get-tuple-element.144, f32[512]{0:T(512)S(1)} %add_rsqrt_fusion, f32[3072]{0:T(1024)S(1)} %copy-done.33, ...), kind=kLoop, calls=%fused_computation.12 | loop fusion | flops 34603008 | bytes 37769216 | tf_op jit(solution)/shard_map/convert_element_type | solution.py:280
  284.0 4.5 convolution_convert_fusion.do_ref
  288.6 14.6 %attend_back.3 = (f32[512,768]{1,0:T(8,128)S(1)}, f32[8,512,256]{2,1,0:T(8,128)}, f32[8,512,256]{2,1,0:T(8,128)}) custom-call(bf16[512,768]{1,0:T(8,128)(2,1)S(1)} %copy.90.q_ref, bf16[512,768]{1,0:T(8,128)(2,1)S(1)} %convolution_convert_fusion.do_ref, bf16[512,768]{1,0:T(8,128)(2,1)} %get-tuple-element.20.o_ref, ...), custom_call_target="tpu_custom_call" | custom-call | flops 32212254720 | bytes 8388608 | tf_op jit(solution)/shard_map/attend_back/pallas_call | solution.py:182
  303.2 8.1 pad_maximum_fusion.1
  311.4 6.0 convolution_convert_fusion.1.do_ref
  317.4 14.5 %attend_back.2 = (f32[512,768]{1,0:T(8,128)S(1)}, f32[8,512,256]{2,1,0:T(8,128)}, f32[8,512,256]{2,1,0:T(8,128)}) custom-call(bf16[512,768]{1,0:T(8,128)(2,1)S(1)} %copy-done.1, bf16[512,768]{1,0:T(8,128)(2,1)S(1)} %convolution_convert_fusion.1.do_ref, bf16[512,768]{1,0:T(8,128)(2,1)} %get-tuple-element.19.o_ref, ...), custom_call_target="tpu_custom_call" | custom-call | flops 32212254720 | bytes 8388608 | tf_op jit(solution)/shard_map/attend_back/pallas_call | solution.py:182
  331.9 8.1 pad_maximum_fusion
  344.5 2.6 multiply_subtract_fusion
  350.1 45.6 %reduce-scatter.9.cloned.1.call-done = f32[1,512,512]{2,1,0:T(8,128)} async-done(((f32[8,512,512]{2,1,0:T(8,128)}), f32[1,512,512]{2,1,0:T(8,128)}) %reduce-scatter.9.cloned.1.call-update) | async-done | bytes 1048592 | tf_op jit(solution)/shard_map/reduce_scatter | solution.py:291
  399.6 53.5 %reduce-scatter.5.cloned.1.call-done = f32[1,512,512]{2,1,0:T(8,128)} async-done(((f32[8,512,512]{2,1,0:T(8,128)}), f32[1,512,512]{2,1,0:T(8,128)}) %reduce-scatter.5.cloned.1.call-update) | async-done | bytes 1048592 | tf_op jit(solution)/shard_map/reduce_scatter | solution.py:291
  462.0 8.6 all-reduce.2
  470.7 5.9 fusion.77
  478.3 3.8 bitcast_add_fusion
  482.3 2.9 fusion.123
  485.2 5.3 fusion.75
  490.6 3.8 bitcast_add_fusion.2
  494.4 10.1 %fusion.12 = f32[768,3072,1]{1,0,2:T(8,128)} fusion(bf16[1,512,3072]{2,1,0:T(8,128)(2,1)} %bitcast.283, bf16[1,512,3072]{2,1,0:T(8,128)(2,1)} %bitcast.284, bf16[1,512,768]{2,1,0:T(8,128)(2,1)} %bitcast.77, bf16[1,512,768]{2,1,0:T(8,128)(2,1)} %bitcast.76), kind=kOutput, calls=%fused_computation.20 | convolution fusion | flops 4835770368 | bytes 17301504 | tf_op jit(solution)/shard_map/ble,bld->ed/dot_general | solution.py:315
  513.3 2.5 fusion.44
  515.9 6.4 fusion.37
  522.4 3.5 fusion.34
  525.9 7.4 fusion.30
  533.5 6.0 fusion.162
  539.5 3.5 reduce-scatter.11.cloned.1.call-done
  543.0 2.6 fusion.54
  545.8 61.3 %reduce-scatter.7.cloned.1.call-done = f32[128,3072]{1,0:T(8,128)} async-done(((f32[512,3072]{1,0:T(8,128)}), f32[128,3072]{1,0:T(8,128)}) %reduce-scatter.7.cloned.1.call-update) | async-done | bytes 1572880 | tf_op jit(solution)/shard_map/reduce_scatter | solution.py:307
  607.1 2.7 fusion.55
  609.9 5.2 pad_maximum_fusion.2
  615.0 23.5 %all-reduce = (f32[6,128]{1,0:T(8,128)}, f32[2,128]{1,0:T(2,128)}, f32[3072]{0:T(1024)}) all-reduce(f32[6,128]{1,0:T(8,128)S(1)} %add.205, f32[2,128]{1,0:T(2,128)S(1)} %add.206, f32[3072]{0:T(1024)S(1)} %add.207), channel_id=1, replica_groups=mesh['dp'=1,'tp'=4,'cp'=8] {'cp'}, use_global_device_ids=true, to_apply=%region_23.24 | all-reduce | flops 4096 | bytes 32768 | tf_op jit(solution)/shard_map/psum | solution.py:319
  638.6 228.4 %all-reduce.5.cloned.1.call-done = (f32[3072,6,128]{0,2,1:T(8,128)}, f32[3072,2,128]{0,2,1:T(8,128)}, f32[3072,2,128]{0,2,1:T(8,128)}, f32[6,128,3072]{2,1,0:T(8,128)}) async-done(((f32[3072,6,128]{0,2,1:T(8,128)}, f32[3072,2,128]{0,2,1:T(8,128)}, f32[3072,2,128]{0,2,1:T(8,128)}, f32[6,128,3072]{2,1,0:T(8,128)}), (f32[3072,6,128]{0,2,1:T(8,128)}, f32[3072,2,128]{0,2,1:T(8,128)}, f32[3072,2,128]{0,2,1:T(8,128)}, ...) | async-done | bytes 25165840 | tf_op jit(solution)/shard_map/psum | solution.py:319
  866.9 9.6 copy.112
  876.5 5.9 copy.113
  882.4 3.3 copy.114
  885.7 19.9 %all-gather.15.cloned.1.call-done = bf16[512,3072]{1,0:T(8,128)(2,1)} async-done(((bf16[128,3072]{1,0:T(8,128)(2,1)}), bf16[512,3072]{1,0:T(8,128)(2,1)}) %all-gather.15.cloned.1.call-update) | async-done | bytes 3145744 | tf_op jit(solution)/shard_map/all_gather | solution.py:310
  905.6 38.6 %all-gather.13.cloned.1.call-done = bf16[512,3072]{1,0:T(8,128)(2,1)} async-done(((bf16[128,3072]{1,0:T(8,128)(2,1)}), bf16[512,3072]{1,0:T(8,128)(2,1)}) %all-gather.13.cloned.1.call-update) | async-done | bytes 3145744 | tf_op jit(solution)/shard_map/all_gather | solution.py:310
  944.1 6.1 pad_maximum_fusion.3
  950.3 8.6 copy.142
  (192 shorter events, 55.2 us)
Async XLA Ops:
  7.2 82.1 %all-gather.9.cloned.1.call-start = ((), (), s32[]{:S(2)}) async-start(), calls=%async_computation.4 | async-start | bytes 4718592 | tf_op jit(solution)/shard_map/all_gather | solution.py:261
  10.9 10.0 %copy-start.9 = (bf16[3072,2,128]{0,2,1:T(8,128)(2,1)}, bf16[3072,2,128]{0,2,1:T(8,128)(2,1)S(1)}, u32[]{:S(2)}) copy-start(bf16[3072,2,128]{0,2,1:T(8,128)(2,1)S(1)} %copy.85) | copy-start | bytes 4718596
  14.8 6.2 copy-start.6
  28.4 22.0 %copy-start.31 = (f32[2,128]{1,0:T(2,128)S(1)}, f32[2,128]{1,0:T(2,128)}, u32[]{:S(2)}) copy-start(f32[2,128]{1,0:T(2,128)} %param.15) | copy-start | bytes 3076
  50.3 15.6 %copy-start.23 = (f32[512,64]{0,1:T(8,128)}, f32[512,64]{0,1:T(8,128)S(1)}, u32[]{:S(2)}) copy-start(f32[512,64]{0,1:T(8,128)S(1)} %get-tuple-element.133) | copy-start | bytes 393220
  53.7 10.1 %copy-start.36 = (f32[6,128]{1,0:T(8,128)S(1)}, f32[6,128]{1,0:T(8,128)}, u32[]{:S(2)}) copy-start(f32[6,128]{1,0:T(8,128)} %param.14) | copy-start | bytes 9220
  58.0 111.6 %all-gather.11.cloned.1.call-start = ((), (), s32[]{:S(2)}) async-start(), calls=%async_computation.5 | async-start | bytes 4718592 | tf_op jit(solution)/shard_map/all_gather | solution.py:261
  58.9 134.7 %all-gather.17.cloned.1.call-start = ((), (), s32[]{:S(2)}) async-start(), calls=%async_computation.12 | async-start | bytes 3932160 | tf_op jit(solution)/shard_map/all_gather | solution.py:269
  62.2 50.3 %collective-permute-start.2 = (bf16[384,3072]{1,0:T(8,128)(2,1)}, bf16[384,3072]{1,0:T(8,128)(2,1)}, u32[]{:S(2)}, u32[]{:S(2)}) collective-permute-start(bf16[384,3072]{1,0:T(8,128)(2,1)} %constant_dynamic-slice_fusion), channel_id=1, source_target_pairs={{0,24},{8,0},{16,8},{24,16},{1,25},{9,1},{17,9},{25,17},{2,26},{10... | collective-permute-start | bytes 7077896 | tf_op jit(solution)/shard_map/ppermute | solution.py:221
  62.2 54.1 %collective-permute-start = (bf16[384,3072]{1,0:T(8,128)(2,1)}, bf16[384,3072]{1,0:T(8,128)(2,1)}, u32[]{:S(2)}, u32[]{:S(2)}) collective-permute-start(bf16[384,3072]{1,0:T(8,128)(2,1)} %constant_dynamic-slice_fusion), channel_id=1, source_target_pairs={{0,8},{8,16},{16,24},{24,0},{1,9},{9,17},{17,25},{25,1},{2,10},{10... | collective-permute-start | bytes 7077896 | tf_op jit(solution)/shard_map/ppermute | solution.py:220
  66.9 32.1 %copy-start = (bf16[512,768]{1,0:T(8,128)(2,1)}, bf16[512,768]{1,0:T(8,128)(2,1)S(1)}, u32[]{:S(2)}) copy-start(bf16[512,768]{1,0:T(8,128)(2,1)S(1)} %copy.89.q_ref) | copy-start | bytes 2359300
  89.3 2.2 copy-start.2
  99.0 134.4 %all-gather.19.cloned.1.call-start = ((), (), s32[]{:S(2)}) async-start(), calls=%async_computation.13 | async-start | bytes 3932160 | tf_op jit(solution)/shard_map/all_gather | solution.py:269
  114.8 31.7 %collective-permute-start.5 = (bf16[192,3072]{1,0:T(8,128)(2,1)}, bf16[192,3072]{1,0:T(8,128)(2,1)}, u32[]{:S(2)}, u32[]{:S(2)}) collective-permute-start(bf16[192,3072]{1,0:T(8,128)(2,1)} %slice.195), channel_id=1, source_target_pairs={{0,24},{8,0},{16,8},{24,16},{1,25},{9,1},{17,9},{25,17},{2,26},{10... | collective-permute-start | bytes 3538952 | tf_op jit(solution)/shard_map/ppermute | solution.py:223
  118.7 36.0 %collective-permute-start.4 = (bf16[192,3072]{1,0:T(8,128)(2,1)}, bf16[192,3072]{1,0:T(8,128)(2,1)}, u32[]{:S(2)}, u32[]{:S(2)}) collective-permute-start(bf16[192,3072]{1,0:T(8,128)(2,1)} %slice.194), channel_id=1, source_target_pairs={{0,8},{8,16},{16,24},{24,0},{1,9},{9,17},{17,25},{25,1},{2,10},{10... | collective-permute-start | bytes 3538952 | tf_op jit(solution)/shard_map/ppermute | solution.py:222
  118.9 74.6 %collective-permute-start.1 = (bf16[384,3072]{1,0:T(8,128)(2,1)}, bf16[384,3072]{1,0:T(8,128)(2,1)}, u32[]{:S(2)}, u32[]{:S(2)}) collective-permute-start(bf16[384,3072]{1,0:T(8,128)(2,1)} %collective-permute-done), channel_id=1, source_target_pairs={{0,1},{1,0},{2,3},{3,2},{4,5},{5,4},{6,7},{7,6},{8,9},{9,8},{10,11... | collective-permute-start | bytes 7077896 | tf_op jit(solution)/shard_map/ppermute | solution.py:226
  157.9 45.2 %collective-permute-start.6 = (bf16[384,3072]{1,0:T(8,128)(2,1)}, bf16[384,3072]{1,0:T(8,128)(2,1)}, u32[]{:S(2)}, u32[]{:S(2)}) collective-permute-start(bf16[384,3072]{1,0:T(8,128)(2,1)} %pad_maximum_fusion.4), channel_id=1, source_target_pairs={{0,1},{1,0},{2,3},{3,2},{4,5},{5,4},{6,7},{7,6},{8,9},{9,8},{10,11... | collective-permute-start | bytes 7077896 | tf_op jit(solution)/shard_map/ppermute | solution.py:226
  169.7 2.2 copy-start.3
  179.4 216.3 %reduce-scatter.9.cloned.1.call-start = ((), (), s32[]{:S(2)}) async-start(), calls=%async_computation.9 | async-start | bytes 9437184 | tf_op jit(solution)/shard_map/reduce_scatter | solution.py:291
  179.5 8.2 slice-start.2
  179.5 8.2 slice-start.3
  179.5 30.8 %collective-permute-start.3 = (bf16[384,3072]{1,0:T(8,128)(2,1)}, bf16[384,3072]{1,0:T(8,128)(2,1)}, u32[]{:S(2)}, u32[]{:S(2)}) collective-permute-start(bf16[384,3072]{1,0:T(8,128)(2,1)} %collective-permute-done.2), channel_id=1, source_target_pairs={{0,1},{1,0},{2,3},{3,2},{4,5},{5,4},{6,7},{7,6},{8,9},{9,8},{10,11... | collective-permute-start | bytes 7077896 | tf_op jit(solution)/shard_map/ppermute | solution.py:226
  193.6 9.5 copy-start.44
  193.6 16.8 %slice-start.8 = ((s8[6291456]{0:T(1024)(128)(4,1)}), s8[4194304]{0:T(1024)(128)(4,1)S(1)}, s32[]{:S(2)}) async-start(s8[6291456]{0:T(1024)(128)(4,1)} %bitcast.275), calls=%async_computation.23 | async-start | bytes 8388608
  203.1 7.3 slice-start.9
  233.4 7.5 copy-start.45
  240.8 23.0 %slice-start = ((s8[6291456]{0:T(1024)(128)(4,1)}), s8[4194304]{0:T(1024)(128)(4,1)S(1)}, s32[]{:S(2)}) async-start(s8[6291456]{0:T(1024)(128)(4,1)} %bitcast.257), calls=%async_computation.15 | async-start | bytes 8388608
  250.1 13.7 %slice-start.1 = ((s8[6291456]{0:T(1024)(128)(4,1)}), s8[2097152]{0:T(1024)(128)(4,1)S(1)}, s32[]{:S(2)}) async-start(s8[6291456]{0:T(1024)(128)(4,1)} %bitcast.257), calls=%async_computation.16 | async-start | bytes 4194304
  250.1 13.7 %copy-start.33 = (f32[3072]{0:T(1024)S(1)}, f32[3072]{0:T(1024)}, u32[]{:S(2)}) copy-start(f32[3072]{0:T(1024)} %param.16) | copy-start | bytes 36868
  263.8 20.2 %slice-start.4 = ((s8[4718592]{0:T(1024)(128)(4,1)}), s8[4194304]{0:T(1024)(128)(4,1)S(1)}, s32[]{:S(2)}) async-start(s8[4718592]{0:T(1024)(128)(4,1)} %bitcast.265), calls=%async_computation.19 | async-start | bytes 8388608
  271.7 12.3 %slice-start.5 = ((s8[4718592]{0:T(1024)(128)(4,1)}), s8[524288]{0:T(1024)(128)(4,1)S(1)}, s32[]{:S(2)}) async-start(s8[4718592]{0:T(1024)(128)(4,1)} %bitcast.265), calls=%async_computation.20 | async-start | bytes 1048576
  311.3 141.8 %reduce-scatter.5.cloned.1.call-start = ((), (), s32[]{:S(2)}) async-start(), calls=%async_computation.6 | async-start | bytes 9437184 | tf_op jit(solution)/shard_map/reduce_scatter | solution.py:291
  311.4 6.0 copy-start.1
  340.1 4.5 copy-start.24
  340.1 4.4 copy-start.28
  340.1 202.9 %reduce-scatter.11.cloned.1.call-start = ((), (), s32[]{:S(2)}) async-start(), calls=%async_computation.10 | async-start | bytes 7864320 | tf_op jit(solution)/shard_map/reduce_scatter | solution.py:307
  342.9 5.9 copy-start.37
  344.5 4.3 copy-start.4
  350.1 109.1 %copy-start.32 = (f32[2,128]{1,0:T(2,128)S(1)}, f32[2,128]{1,0:T(2,128)}, u32[]{:S(2)}) copy-start(f32[2,128]{1,0:T(2,128)} %param.15) | copy-start | bytes 3076
  458.5 2.2 copy-start.19
  470.7 6.0 copy-start.5
  470.7 6.0 copy-start.10
  470.7 6.0 copy-start.20
  470.7 6.0 copy-start.22
  482.2 3.0 copy-start.42
  482.2 124.9 %reduce-scatter.7.cloned.1.call-start = ((), (), s32[]{:S(2)}) async-start(), calls=%async_computation.7 | async-start | bytes 7864320 | tf_op jit(solution)/shard_map/reduce_scatter | solution.py:307
  482.2 2.9 copy-start.15
  482.2 2.9 copy-start.17
  485.2 5.4 copy-start.8
  485.2 5.4 copy-start.27
  494.4 372.6 %all-reduce.5.cloned.1.call-start = ((), (), s32[]{:S(2)}) async-start(), calls=%async_computation.14 | async-start | bytes 50331648 | tf_op jit(solution)/shard_map/psum | solution.py:319
  504.6 8.8 copy-start.43
  513.3 9.0 slice-start.6
  515.9 6.4 slice-start.7
  515.9 6.4 copy-start.29
  515.9 6.4 copy-start.30
  533.4 372.2 %all-gather.15.cloned.1.call-start = ((), (), s32[]{:S(2)}) async-start(), calls=%async_computation.11 | async-start | bytes 3932160 | tf_op jit(solution)/shard_map/all_gather | solution.py:310
  539.5 70.3 %copy-start.34 = (f32[3072]{0:T(1024)S(1)}, f32[3072]{0:T(1024)}, u32[]{:S(2)}) copy-start(f32[3072]{0:T(1024)} %get-tuple-element.58) | copy-start | bytes 36868
  539.5 70.3 %copy-start.35 = (f32[3072]{0:T(1024)S(1)}, f32[3072]{0:T(1024)}, u32[]{:S(2)}) copy-start(f32[3072]{0:T(1024)} %get-tuple-element.61) | copy-start | bytes 36868
  539.5 70.4 %copy-start.38 = (f32[6,128]{1,0:T(8,128)S(1)}, f32[6,128]{1,0:T(8,128)}, u32[]{:S(2)}) copy-start(f32[6,128]{1,0:T(8,128)} %get-tuple-element.64) | copy-start | bytes 9220
  539.5 70.4 %copy-start.39 = (f32[6,128]{1,0:T(8,128)S(1)}, f32[6,128]{1,0:T(8,128)}, u32[]{:S(2)}) copy-start(f32[6,128]{1,0:T(8,128)} %get-tuple-element.67) | copy-start | bytes 9220
  539.5 70.4 %copy-start.11 = (bf16[1,512,3072]{2,1,0:T(8,128)(2,1)S(1)}, bf16[1,512,3072]{2,1,0:T(8,128)(2,1)}, u32[]{:S(2)}) copy-start(bf16[1,512,3072]{2,1,0:T(8,128)(2,1)} %get-tuple-element.90) | copy-start | bytes 9437188
  545.7 398.5 %all-gather.13.cloned.1.call-start = ((), (), s32[]{:S(2)}) async-start(), calls=%async_computation.8 | async-start | bytes 3932160 | tf_op jit(solution)/shard_map/all_gather | solution.py:310
  876.5 5.9 copy-start.25
  (10 other events, 12.5 us)
Sparse Core Ops, SparseCore 0:
  58.2 31.0 all-gather.8
  91.5 29.1 all-gather.10
  122.2 50.9 all-gather.16
  179.5 53.8 all-gather.18
  311.5 84.2 reduce-scatter.8
  398.5 54.6 reduce-scatter.4
  482.3 60.6 reduce-scatter.10
  545.9 61.1 reduce-scatter.6
  610.4 256.4 all-reduce.4
  868.9 36.5 all-gather.14
  907.1 36.9 all-gather.12
